TPU v7x, 256 devices: a whole 4x4x8 slice. The times are simulated.
256 devices in a mesh: gx: 8 (over y, x_lo), gy: 16 (over z, core), gz: 2 (over x_hi).
Axes of the slice: x: 4 (x_hi: 2, x_lo: 2; x = x_hi * 2 + x_lo), y: 4, z: 8, core: 2. Of those that a mesh axis runs over, the one named last changes fastest.
Arguments:
- starting_kelvin: float32 [16, 128, 4096], P(None, 'gx', ('gy', 'gz')), may hold values from -6 to 6
- substance_label: int32 [16, 128, 4096], P(None, 'gx', ('gy', 'gz')), may hold values from 0 to 3
- voxel_source_patch: int32 [16, 128, 4096], P(None, 'gx', ('gy', 'gz')), may hold values from 0 to 15
- substance_traits: float32 [4, 4], replicated, may hold values from 0.5 to 2
- patch_source_intensity: float32 [16], replicated, may hold values from 0 to 8
Outputs:
- warmed_result: float32 [16, 128, 4096], P(None, 'gx', ('gy', 'gz'))
- solution: float32 [3, 16, 128, 4096], P(None, 'gz', 'gx', 'gy')
- residual: float32 [3, 16, 128, 4096], P(None, 'gz', 'gx', 'gy')
All inputs are finite; a program needn't handle non-finite values.
Results may differ from a plain program's by a relative error of at most 0.0029.
Values sent between devices are 32-bit elements; how exact they have to be, the bound alone decides.
A program may use at most 64 MiB of HBM per device.

v0:
```python
import jax
import jax.numpy as jnp
from jax import lax
from jax.sharding import Mesh
from jax.sharding import PartitionSpec as P

HEAT_STEPS = 2
ITERS = 3
GX_GY_GZ = ("gx_0", "gx_1", "gy_0", "gy_1", "gz")
GX = ("gx_0", "gx_1")
GY_GZ = ("gy_0", "gy_1", "gz")
GY = ("gy_0", "gy_1")


time_step = 0.03
anchor_scale = 0.5
strain_gain = 2.0


def over_axes(value, axes):
    for axis in axes:
        value = lax.psum(value, axis)
    return value


def padded(value, sides, width):
    for axis, dim in sides:
        devices, length = (lax.axis_size(axis), value.shape[dim])
        up = [(i, (i + 1) % devices) for i in range(devices - 1)]
        down = [(j, i) for i, j in up]
        last = lax.slice_in_dim(value, length - width, length, axis=dim)
        initial = lax.slice_in_dim(value, 0, width, axis=dim)
        before = lax.ppermute(last, axis, up)
        after = lax.ppermute(initial, axis, down)
        value = jnp.concatenate([before, value, after], axis=dim)
    return value


def lookup(identity, table, count):
    summed = jnp.zeros(identity.shape, jnp.float32)
    for number in range(count):
        summed = summed + jnp.where(identity == number, table[number], jnp.float32(0.0))
    return summed


def conduct(own, other):
    return 2.0 * own * other / jnp.maximum(own + other, 0.25)


def heat_step(padded_temp, padded_cond, power, inverse_cap):
    centre = padded_temp[:, 1:-1, 1:-1]
    own = padded_cond[:, 1:-1, 1:-1]
    layers, rows, columns = centre.shape
    heat_flux = jnp.zeros_like(centre)
    for row_offset, column_offset in ((0, 1), (2, 1), (1, 0), (1, 2)):
        neighbour = padded_temp[
            :, row_offset : row_offset + rows, column_offset : column_offset + columns
        ]
        other = padded_cond[
            :, row_offset : row_offset + rows, column_offset : column_offset + columns
        ]
        heat_flux = heat_flux + conduct(own, other) * (neighbour - centre)
    vertical_temp = jnp.pad(centre, ((1, 1), (0, 0), (0, 0)))
    vertical_cond = jnp.pad(own, ((1, 1), (0, 0), (0, 0)))
    for layer_offset in (0, 2):
        other = vertical_cond[layer_offset : layer_offset + layers]
        neighbour = vertical_temp[layer_offset : layer_offset + layers]
        heat_flux = heat_flux + conduct(own, other) * (neighbour - centre)
    return centre + time_step * inverse_cap * (heat_flux + power)


def crop(array, margin):
    return array[:, margin : array.shape[1] - margin, margin : array.shape[2] - margin]


def neighbour_offsets():
    listed = []
    for along_z in (-1, 0, 1):
        for along_x in (-1, 0, 1):
            for along_y in (-1, 0, 1):
                if along_z != 0 or along_x != 0 or along_y != 0:
                    listed.append((along_z, along_x, along_y))
    return listed


def apply_operator(field, padded_field, modulus, padded_modulus):
    layers, rows, columns = modulus.shape
    parts = [
        anchor_scale * modulus * field[0],
        anchor_scale * modulus * field[1],
        anchor_scale * modulus * field[2],
    ]
    for along_z, along_x, along_y in neighbour_offsets():
        length_sq = along_z * along_z + along_x * along_x + along_y * along_y
        window = (
            slice(1 + along_z, 1 + along_z + layers),
            slice(1 + along_x, 1 + along_x + rows),
            slice(1 + along_y, 1 + along_y + columns),
        )
        weight = 0.5 / length_sq * (modulus + padded_modulus[window])
        change = [field[index_c] - padded_field[index_c][window] for index_c in range(3)]
        projected = (along_z * change[0] + along_x * change[1] + along_y * change[2]) / length_sq
        for index_c, direction_part in enumerate((along_z, along_x, along_y)):
            parts[index_c] = parts[index_c] + weight * (
                0.5 * change[index_c] + direction_part * projected
            )
    return jnp.stack(parts)


def thermal_load(modulus, padded_modulus, strain, padded_strain):
    layers, rows, columns = modulus.shape
    parts = [jnp.zeros_like(modulus), jnp.zeros_like(modulus), jnp.zeros_like(modulus)]
    for along_z, along_x, along_y in neighbour_offsets():
        length_sq = along_z * along_z + along_x * along_x + along_y * along_y
        window = (
            slice(1 + along_z, 1 + along_z + layers),
            slice(1 + along_x, 1 + along_x + rows),
            slice(1 + along_y, 1 + along_y + columns),
        )
        weight = 0.5 / length_sq * (modulus + padded_modulus[window])
        pushing = weight * (0.5 * (strain + padded_strain[window]))
        for index_c, direction_part in enumerate((along_z, along_x, along_y)):
            if direction_part != 0:
                parts[index_c] = parts[index_c] - strain_gain * direction_part * pushing
    return jnp.stack(parts)


def two_products(residual, image):
    return (
        over_axes(jnp.sum(residual * residual), GX_GY_GZ),
        over_axes(jnp.sum(residual * image), GX_GY_GZ),
    )


def per_device(
    starting_kelvin, substance_label, voxel_source_patch, substance_traits, patch_source_intensity
):
    count = substance_traits.shape[1]
    diffusive_coefficient = lookup(substance_label, substance_traits[0], count)
    inverse_cap = 1.0 / lookup(substance_label, substance_traits[1], count)
    power = lookup(voxel_source_patch, patch_source_intensity, patch_source_intensity.shape[0])
    padded_array = padded(
        jnp.stack([starting_kelvin, diffusive_coefficient, power, inverse_cap]),
        ((GX, 2), (GY_GZ, 3)),
        HEAT_STEPS,
    )
    warmed_result = padded_array[0]
    for number in range(HEAT_STEPS):
        warmed_result = heat_step(
            warmed_result,
            crop(padded_array[1], number),
            crop(padded_array[2], number + 1),
            crop(padded_array[3], number + 1),
        )
    modulus = lookup(substance_label, substance_traits[2], count)
    strain = lookup(substance_label, substance_traits[3], count) * warmed_result
    fields = jnp.stack([modulus, strain])
    fields = lax.all_to_all(fields, "gz", split_axis=1, concat_axis=3, tiled=True)
    padded_fields = padded(fields, ((GX, 2), (GY, 3), ("gz", 1)), 1)

    def extend(field):
        return padded(field, ((GX, 2), (GY, 3), ("gz", 1)), 1)

    modulus = fields[0]
    padded_modulus = padded_fields[0]
    load = thermal_load(modulus, padded_modulus, fields[1], padded_fields[1])

    def operate(field):
        return apply_operator(field, extend(field), modulus, padded_modulus)

    solution = jnp.zeros_like(load)
    residual = load
    image = operate(residual)
    norm_now, product = two_products(residual, image)
    alpha = norm_now / product
    direction, along_image = (residual, image)
    for number in range(ITERS):
        solution = solution + alpha * direction
        residual = residual - alpha * along_image
        if number + 1 < ITERS:
            image = operate(residual)
            norm_next, product = two_products(residual, image)
            ratio = norm_next / norm_now
            alpha = norm_next / (product - ratio * norm_next / alpha)
            direction = residual + ratio * direction
            along_image = image + ratio * along_image
            norm_now = norm_next
    return (warmed_result, solution, residual)


def solution(mesh):
    split = Mesh(
        mesh.devices.reshape(4, 2, 8, 2, mesh.shape["gz"]), ("gx_0", "gx_1", "gy_0", "gy_1", "gz")
    )
    placed = (P(None, GX, GY_GZ), P(None, GX, GY_GZ), P(None, GX, GY_GZ), P(), P())
    return jax.shard_map(
        per_device,
        mesh=split,
        in_specs=placed,
        out_specs=(P(None, GX, GY_GZ), P(None, "gz", GX, GY), P(None, "gz", GX, GY)),
        check_vma=False,
    )
```

profile of v0, /device:TPU:1, one launch (start us, length us, event | category | flops | bytes accessed | tf_op | source)
XLA Modules:
  0.0 349.6 jit_solution(3957960679545552829)
XLA Ops:
  8.0 5.2 %add_bitcast_fusion.11 = (f32[1,16,16,128]{3,1,2,0:T(8,128)S(1)}, f32[1,16,16,128]{3,1,2,0:T(8,128)S(1)}) fusion(pred[16,16,128]{2,0,1:T(8,128)(4,1)S(1)} %get-tuple-element.98, pred[16,16,128]{2,0,1:T(8,128)(4,1)S(1)} %get-tuple-element.97, pred[16,16,128]{2,0,1:T(8,128)(4,1)S(1)} %get-tuple-element.96, pred[16,16,128]{2,0,1:T(8,128)(4,1)S(1)} %get-tuple-element.95, ...), kind=kLoop, calls=%fused_computation.621 | loop fusion | flops 491520 | bytes 393248 | tf_op jit(solution)/shard_map/stack | solution.py:143
  13.2 11.3 %copy_bitcast_fusion = (f32[1,16,16,128]{3,1,2,0:T(8,128)S(1)}, f32[1,16,16,128]{3,1,2,0:T(8,128)S(1)}) fusion(f32[16,16,128]{2,1,0:T(8,128)} %param.5, f32[]{:T(128)} %bitcast.21, f32[]{:T(128)} %bitcast.20, f32[]{:T(128)} %bitcast.19, f32[]{:T(128)} %bitcast.18, f32[]{:T(128)} %bitcast.17, f32[]{:T(128)} %bitcast.16, f32[]{:T(128)} %bitcast.15, ...), kind=kLoop, calls=%fused_computation.521 | loop fusion | flops 1540096 | bytes 524352 | tf_op jit(solution)/shard_map/stack | solution.py:143
  34.2 4.5 %collective-permute-start.2 = (f32[4,16,20,2]{2,1,3,0:T(8,128)S(1)}, f32[4,16,20,2]{2,1,3,0:T(8,128)S(1)}, u32[]{:S(2)}, u32[]{:S(2)}) collective-permute-start(f32[4,16,20,2]{2,1,3,0:T(8,128)S(1)} %copy.202), channel_id=1, source_target_pairs={{0,1},{1,2},{2,3},{3,4},{4,5},{5,6},{6,7},{7,8},{8,9},{9,10},{10,1... | collective-permute-start | bytes 30728 | tf_op jit(solution)/shard_map/ppermute | solution.py:33
  52.1 12.7 %all_to_all.18 = f32[2,16,16,128]{3,2,0,1:T(8,128)S(1)} all-to-all(f32[2,16,16,128]{3,2,0,1:T(8,128)S(1)} %copy.206), channel_id=1, replica_groups=mesh['gx_0'=4,'gx_1'=2,'gy_0'=8,'gy_1'=2,'gz'=2] {'gz'}, dimensions={1} | all-to-all | bytes 524288 | tf_op jit(solution)/shard_map/all_to_all | solution.py:158
  73.4 5.2 %collective-permute-start.6 = (f32[2,8,18,1]{3,2,1,0:T(8,128)S(1)}, f32[2,8,18,1]{3,2,1,0:T(8,128)S(1)}, u32[]{:S(2)}, u32[]{:S(2)}) collective-permute-start(f32[2,8,18,1]{3,2,1,0:T(8,128)S(1)} %get-tuple-element.142), channel_id=1, source_target_pairs={{0,2},{2,4},{4,6},{6,8},{8,10},{10,12},{12,14},{14,16},{16,18},{18... | collective-permute-start | bytes 3464 | tf_op jit(solution)/shard_map/ppermute | solution.py:33
  81.2 4.4 %collective-permute-done.7 = f32[2,8,18,1]{3,2,1,0:T(8,128)S(1)} collective-permute-done((f32[2,8,18,1]{3,2,1,0:T(8,128)S(1)}, f32[2,8,18,1]{3,2,1,0:T(8,128)S(1)}, u32[]{:S(2)}, u32[]{:S(2)}) %collective-permute-start.7) | collective-permute-done | bytes 1184 | tf_op jit(solution)/shard_map/ppermute | solution.py:34
  89.5 4.8 %collective-permute-done.9 = f32[2,1,18,258]{3,2,1,0:T(8,128)S(1)} collective-permute-done((f32[2,1,18,258]{3,2,1,0:T(8,128)S(1)}, f32[2,1,18,258]{3,2,1,0:T(8,128)S(1)}, u32[]{:S(2)}, u32[]{:S(2)}) %collective-permute-start.9) | collective-permute-done | bytes 37184 | tf_op jit(solution)/shard_map/ppermute | solution.py:34
  121.6 5.3 %collective-permute-done.15 = f32[3,1,18,258]{3,2,1,0:T(8,128)S(1)} collective-permute-done((f32[3,1,18,258]{3,2,1,0:T(8,128)S(1)}, f32[3,1,18,258]{3,2,1,0:T(8,128)S(1)}, u32[]{:S(2)}, u32[]{:S(2)}) %collective-permute-start.15) | collective-permute-done | bytes 55760 | tf_op jit(solution)/shard_map/ppermute | solution.py:34
  136.0 7.9 %all-reduce.9 = (f32[]{:T(128)}, f32[]{:T(128)}) all-reduce(f32[]{:T(128)} %get-tuple-element.17, f32[]{:T(128)} %get-tuple-element.16), channel_id=1, replica_groups=mesh['gx_0'=4,'gx_1'=2,'gy_0'=8,'gy_1'=2,'gz'=2] {'gx_0'}, use_global_device_ids=true, to_apply=%region_1.2 | all-reduce | flops 2 | bytes 16 | tf_op jit(solution)/shard_map/psum | solution.py:22
  148.2 17.7 %all-reduce.6 = (f32[]{:T(128)}, f32[]{:T(128)}) all-reduce(f32[]{:T(128)} %get-tuple-element.46, f32[]{:T(128)} %get-tuple-element.47), channel_id=1, replica_groups=mesh['gx_0'=4,'gx_1'=2,'gy_0'=8,'gy_1'=2,'gz'=2] {'gy_0'}, use_global_device_ids=true, to_apply=%region_3.4 | all-reduce | flops 2 | bytes 16 | tf_op jit(solution)/shard_map/psum | solution.py:22
  166.0 8.6 %all-reduce.15 = (f32[]{:T(128)}, f32[]{:T(128)}) all-reduce(f32[]{:T(128)} %get-tuple-element.22, f32[]{:T(128)} %get-tuple-element.23), channel_id=1, replica_groups=mesh['gx_0'=4,'gx_1'=2,'gy_0'=8,'gy_1'=2,'gz'=2] {'gy_1'}, use_global_device_ids=true, to_apply=%region_4.5 | all-reduce | flops 2 | bytes 16 | tf_op jit(solution)/shard_map/psum | solution.py:22
  174.5 5.9 %all-reduce.12 = (f32[]{:T(128)}, f32[]{:T(128)}) all-reduce(f32[]{:T(128)} %get-tuple-element.40, f32[]{:T(128)} %get-tuple-element.41), channel_id=1, replica_groups=mesh['gx_0'=4,'gx_1'=2,'gy_0'=8,'gy_1'=2,'gz'=2] {'gz'}, use_global_device_ids=true, to_apply=%region_5.6 | all-reduce | flops 2 | bytes 16 | tf_op jit(solution)/shard_map/psum | solution.py:22
  190.4 5.2 %collective-permute-start.18 = (f32[3,8,18,1]{3,2,1,0:T(8,128)S(1)}, f32[3,8,18,1]{3,2,1,0:T(8,128)S(1)}, u32[]{:S(2)}, u32[]{:S(2)}) collective-permute-start(f32[3,8,18,1]{3,2,1,0:T(8,128)S(1)} %get-tuple-element.128), channel_id=1, source_target_pairs={{0,2},{2,4},{4,6},{6,8},{8,10},{10,12},{12,14},{14,16},{16,18},{18... | collective-permute-start | bytes 5192 | tf_op jit(solution)/shard_map/ppermute | solution.py:33
  207.7 5.3 %collective-permute-done.21 = f32[3,1,18,258]{3,2,1,0:T(8,128)S(1)} collective-permute-done((f32[3,1,18,258]{3,2,1,0:T(8,128)S(1)}, f32[3,1,18,258]{3,2,1,0:T(8,128)S(1)}, u32[]{:S(2)}, u32[]{:S(2)}) %collective-permute-start.21) | collective-permute-done | bytes 55760 | tf_op jit(solution)/shard_map/ppermute | solution.py:34
  220.2 7.1 %all-reduce.8 = (f32[]{:T(128)}, f32[]{:T(128)}) all-reduce(f32[]{:T(128)} %get-tuple-element.15, f32[]{:T(128)} %get-tuple-element.14), channel_id=1, replica_groups=mesh['gx_0'=4,'gx_1'=2,'gy_0'=8,'gy_1'=2,'gz'=2] {'gx_0'}, use_global_device_ids=true, to_apply=%region_13.14 | all-reduce | flops 2 | bytes 16 | tf_op jit(solution)/shard_map/psum | solution.py:22
  231.7 14.0 %all-reduce.5 = (f32[]{:T(128)}, f32[]{:T(128)}) all-reduce(f32[]{:T(128)} %get-tuple-element.44, f32[]{:T(128)} %get-tuple-element.45), channel_id=1, replica_groups=mesh['gx_0'=4,'gx_1'=2,'gy_0'=8,'gy_1'=2,'gz'=2] {'gy_0'}, use_global_device_ids=true, to_apply=%region_15.16 | all-reduce | flops 2 | bytes 16 | tf_op jit(solution)/shard_map/psum | solution.py:22
  245.7 9.5 %all-reduce.14 = (f32[]{:T(128)}, f32[]{:T(128)}) all-reduce(f32[]{:T(128)} %get-tuple-element.20, f32[]{:T(128)} %get-tuple-element.21), channel_id=1, replica_groups=mesh['gx_0'=4,'gx_1'=2,'gy_0'=8,'gy_1'=2,'gz'=2] {'gy_1'}, use_global_device_ids=true, to_apply=%region_16.17 | all-reduce | flops 2 | bytes 16 | tf_op jit(solution)/shard_map/psum | solution.py:22
  255.2 6.1 %all-reduce.11 = (f32[]{:T(128)}, f32[]{:T(128)}) all-reduce(f32[]{:T(128)} %get-tuple-element.38, f32[]{:T(128)} %get-tuple-element.39), channel_id=1, replica_groups=mesh['gx_0'=4,'gx_1'=2,'gy_0'=8,'gy_1'=2,'gz'=2] {'gz'}, use_global_device_ids=true, to_apply=%region_17.18 | all-reduce | flops 2 | bytes 16 | tf_op jit(solution)/shard_map/psum | solution.py:22
  273.8 5.0 %collective-permute-start.24 = (f32[3,8,18,1]{3,2,1,0:T(8,128)S(1)}, f32[3,8,18,1]{3,2,1,0:T(8,128)S(1)}, u32[]{:S(2)}, u32[]{:S(2)}) collective-permute-start(f32[3,8,18,1]{3,2,1,0:T(8,128)S(1)} %get-tuple-element.126), channel_id=1, source_target_pairs={{0,2},{2,4},{4,6},{6,8},{8,10},{10,12},{12,14},{14,16},{16,18},{18... | collective-permute-start | bytes 5192 | tf_op jit(solution)/shard_map/ppermute | solution.py:33
  290.8 5.0 %collective-permute-done.27 = f32[3,1,18,258]{3,2,1,0:T(8,128)S(1)} collective-permute-done((f32[3,1,18,258]{3,2,1,0:T(8,128)S(1)}, f32[3,1,18,258]{3,2,1,0:T(8,128)S(1)}, u32[]{:S(2)}, u32[]{:S(2)}) %collective-permute-start.27) | collective-permute-done | bytes 55760 | tf_op jit(solution)/shard_map/ppermute | solution.py:34
  303.1 7.6 %all-reduce.7 = (f32[]{:T(128)}, f32[]{:T(128)}) all-reduce(f32[]{:T(128)} %get-tuple-element.13, f32[]{:T(128)} %get-tuple-element.12), channel_id=1, replica_groups=mesh['gx_0'=4,'gx_1'=2,'gy_0'=8,'gy_1'=2,'gz'=2] {'gx_0'}, use_global_device_ids=true, to_apply=%region_25.26 | all-reduce | flops 2 | bytes 16 | tf_op jit(solution)/shard_map/psum | solution.py:22
  315.1 14.0 %all-reduce.4 = (f32[]{:T(128)}, f32[]{:T(128)}) all-reduce(f32[]{:T(128)} %get-tuple-element.42, f32[]{:T(128)} %get-tuple-element.43), channel_id=1, replica_groups=mesh['gx_0'=4,'gx_1'=2,'gy_0'=8,'gy_1'=2,'gz'=2] {'gy_0'}, use_global_device_ids=true, to_apply=%region_27.28 | all-reduce | flops 2 | bytes 16 | tf_op jit(solution)/shard_map/psum | solution.py:22
  329.1 9.5 %all-reduce.13 = (f32[]{:T(128)}, f32[]{:T(128)}) all-reduce(f32[]{:T(128)} %get-tuple-element.18, f32[]{:T(128)} %get-tuple-element.19), channel_id=1, replica_groups=mesh['gx_0'=4,'gx_1'=2,'gy_0'=8,'gy_1'=2,'gz'=2] {'gy_1'}, use_global_device_ids=true, to_apply=%region_28.29 | all-reduce | flops 2 | bytes 16 | tf_op jit(solution)/shard_map/psum | solution.py:22
  338.7 5.9 %all-reduce.10 = (f32[]{:T(128)}, f32[]{:T(128)}) all-reduce(f32[]{:T(128)} %get-tuple-element.36, f32[]{:T(128)} %get-tuple-element.37), channel_id=1, replica_groups=mesh['gx_0'=4,'gx_1'=2,'gy_0'=8,'gy_1'=2,'gz'=2] {'gz'}, use_global_device_ids=true, to_apply=%region_29.30 | all-reduce | flops 2 | bytes 16 | tf_op jit(solution)/shard_map/psum | solution.py:22
  (121 shorter events, 150.9 us)
Async XLA Ops:
  24.5 5.3 %collective-permute-start = (f32[4,16,2,128]{3,1,2,0:T(8,128)S(1)}, f32[4,16,2,128]{3,1,2,0:T(8,128)S(1)}, u32[]{:S(2)}, u32[]{:S(2)}) collective-permute-start(f32[4,16,2,128]{3,1,2,0:T(8,128)S(1)} %get-tuple-element.132), channel_id=1, source_target_pairs={{0,32},{32,64},{64,96},{96,128},{128,160},{160,192},{192,224},{1,3... | collective-permute-start | bytes 196616 | tf_op jit(solution)/shard_map/ppermute | solution.py:33
  28.4 5.0 %collective-permute-start.1 = (f32[4,16,2,128]{3,1,2,0:T(8,128)S(1)}, f32[4,16,2,128]{3,1,2,0:T(8,128)S(1)}, u32[]{:S(2)}, u32[]{:S(2)}) collective-permute-start(f32[4,16,2,128]{3,1,2,0:T(8,128)S(1)} %get-tuple-element.133), channel_id=1, source_target_pairs={{32,0},{64,32},{96,64},{128,96},{160,128},{192,160},{224,192},{33,... | collective-permute-start | bytes 196616 | tf_op jit(solution)/shard_map/ppermute | solution.py:34
  34.2 8.8 %collective-permute-start.2 = (f32[4,16,20,2]{2,1,3,0:T(8,128)S(1)}, f32[4,16,20,2]{2,1,3,0:T(8,128)S(1)}, u32[]{:S(2)}, u32[]{:S(2)}) collective-permute-start(f32[4,16,20,2]{2,1,3,0:T(8,128)S(1)} %copy.202), channel_id=1, source_target_pairs={{0,1},{1,2},{2,3},{3,4},{4,5},{5,6},{6,7},{7,8},{8,9},{9,10},{10,1... | collective-permute-start | bytes 30728 | tf_op jit(solution)/shard_map/ppermute | solution.py:33
  39.2 7.3 %collective-permute-start.3 = (f32[4,16,20,2]{2,1,3,0:T(8,128)S(1)}, f32[4,16,20,2]{2,1,3,0:T(8,128)S(1)}, u32[]{:S(2)}, u32[]{:S(2)}) collective-permute-start(f32[4,16,20,2]{2,1,3,0:T(8,128)S(1)} %copy.203), channel_id=1, source_target_pairs={{1,0},{2,1},{3,2},{4,3},{5,4},{6,5},{7,6},{8,7},{9,8},{10,9},{11,1... | collective-permute-start | bytes 30728 | tf_op jit(solution)/shard_map/ppermute | solution.py:34
  65.2 4.8 %collective-permute-start.4 = (f32[2,8,1,256]{3,2,1,0:T(1,128)S(1)}, f32[2,8,1,256]{3,2,1,0:T(1,128)S(1)}, u32[]{:S(2)}, u32[]{:S(2)}) collective-permute-start(f32[2,8,1,256]{3,2,1,0:T(1,128)S(1)} %get-tuple-element.146), channel_id=1, source_target_pairs={{0,32},{32,64},{64,96},{96,128},{128,160},{160,192},{192,224},{1,3... | collective-permute-start | bytes 49160 | tf_op jit(solution)/shard_map/ppermute | solution.py:33
  68.7 4.5 %collective-permute-start.5 = (f32[2,8,1,256]{3,2,1,0:T(1,128)S(1)}, f32[2,8,1,256]{3,2,1,0:T(1,128)S(1)}, u32[]{:S(2)}, u32[]{:S(2)}) collective-permute-start(f32[2,8,1,256]{3,2,1,0:T(1,128)S(1)} %get-tuple-element.147), channel_id=1, source_target_pairs={{32,0},{64,32},{96,64},{128,96},{160,128},{192,160},{224,192},{33,... | collective-permute-start | bytes 49160 | tf_op jit(solution)/shard_map/ppermute | solution.py:34
  73.4 7.8 %collective-permute-start.6 = (f32[2,8,18,1]{3,2,1,0:T(8,128)S(1)}, f32[2,8,18,1]{3,2,1,0:T(8,128)S(1)}, u32[]{:S(2)}, u32[]{:S(2)}) collective-permute-start(f32[2,8,18,1]{3,2,1,0:T(8,128)S(1)} %get-tuple-element.142), channel_id=1, source_target_pairs={{0,2},{2,4},{4,6},{6,8},{8,10},{10,12},{12,14},{14,16},{16,18},{18... | collective-permute-start | bytes 3464 | tf_op jit(solution)/shard_map/ppermute | solution.py:33
  78.6 7.0 %collective-permute-start.7 = (f32[2,8,18,1]{3,2,1,0:T(8,128)S(1)}, f32[2,8,18,1]{3,2,1,0:T(8,128)S(1)}, u32[]{:S(2)}, u32[]{:S(2)}) collective-permute-start(f32[2,8,18,1]{3,2,1,0:T(8,128)S(1)} %get-tuple-element.143), channel_id=1, source_target_pairs={{2,0},{4,2},{6,4},{8,6},{10,8},{12,10},{14,12},{16,14},{18,16},{20... | collective-permute-start | bytes 3464 | tf_op jit(solution)/shard_map/ppermute | solution.py:34
  87.7 6.6 %collective-permute-start.9 = (f32[2,1,18,258]{3,2,1,0:T(8,128)S(1)}, f32[2,1,18,258]{3,2,1,0:T(8,128)S(1)}, u32[]{:S(2)}, u32[]{:S(2)}) collective-permute-start(f32[2,1,18,258]{3,2,1,0:T(8,128)S(1)} %get-tuple-element.123), channel_id=1, source_target_pairs={{1,0},{3,2},{5,4},{7,6},{9,8},{11,10},{13,12},{15,14},{17,16},{19,... | collective-permute-start | bytes 111464 | tf_op jit(solution)/shard_map/ppermute | solution.py:34
  97.4 4.4 %collective-permute-start.10 = (f32[3,8,1,256]{3,2,1,0:T(1,128)S(1)}, f32[3,8,1,256]{3,2,1,0:T(1,128)S(1)}, u32[]{:S(2)}, u32[]{:S(2)}) collective-permute-start(f32[3,8,1,256]{3,2,1,0:T(1,128)S(1)} %get-tuple-element.140), channel_id=1, source_target_pairs={{0,32},{32,64},{64,96},{96,128},{128,160},{160,192},{192,224},{1,3... | collective-permute-start | bytes 73736 | tf_op jit(solution)/shard_map/ppermute | solution.py:33
  100.5 4.6 %collective-permute-start.11 = (f32[3,8,1,256]{3,2,1,0:T(1,128)S(1)}, f32[3,8,1,256]{3,2,1,0:T(1,128)S(1)}, u32[]{:S(2)}, u32[]{:S(2)}) collective-permute-start(f32[3,8,1,256]{3,2,1,0:T(1,128)S(1)} %get-tuple-element.141), channel_id=1, source_target_pairs={{32,0},{64,32},{96,64},{128,96},{160,128},{192,160},{224,192},{33,... | collective-permute-start | bytes 73736 | tf_op jit(solution)/shard_map/ppermute | solution.py:34
  105.3 8.0 %collective-permute-start.12 = (f32[3,8,18,1]{3,2,1,0:T(8,128)S(1)}, f32[3,8,18,1]{3,2,1,0:T(8,128)S(1)}, u32[]{:S(2)}, u32[]{:S(2)}) collective-permute-start(f32[3,8,18,1]{3,2,1,0:T(8,128)S(1)} %get-tuple-element.130), channel_id=1, source_target_pairs={{0,2},{2,4},{4,6},{6,8},{8,10},{10,12},{12,14},{14,16},{16,18},{18... | collective-permute-start | bytes 5192 | tf_op jit(solution)/shard_map/ppermute | solution.py:33
  109.7 8.0 %collective-permute-start.13 = (f32[3,8,18,1]{3,2,1,0:T(8,128)S(1)}, f32[3,8,18,1]{3,2,1,0:T(8,128)S(1)}, u32[]{:S(2)}, u32[]{:S(2)}) collective-permute-start(f32[3,8,18,1]{3,2,1,0:T(8,128)S(1)} %get-tuple-element.131), channel_id=1, source_target_pairs={{2,0},{4,2},{6,4},{8,6},{10,8},{12,10},{14,12},{16,14},{18,16},{20... | collective-permute-start | bytes 5192 | tf_op jit(solution)/shard_map/ppermute | solution.py:34
  119.9 7.0 %collective-permute-start.15 = (f32[3,1,18,258]{3,2,1,0:T(8,128)S(1)}, f32[3,1,18,258]{3,2,1,0:T(8,128)S(1)}, u32[]{:S(2)}, u32[]{:S(2)}) collective-permute-start(f32[3,1,18,258]{3,2,1,0:T(8,128)S(1)} %get-tuple-element.119), channel_id=1, source_target_pairs={{1,0},{3,2},{5,4},{7,6},{9,8},{11,10},{13,12},{15,14},{17,16},{19,... | collective-permute-start | bytes 167192 | tf_op jit(solution)/shard_map/ppermute | solution.py:34
  181.9 5.0 %collective-permute-start.16 = (f32[3,8,1,256]{3,2,1,0:T(1,128)S(1)}, f32[3,8,1,256]{3,2,1,0:T(1,128)S(1)}, u32[]{:S(2)}, u32[]{:S(2)}) collective-permute-start(f32[3,8,1,256]{3,2,1,0:T(1,128)S(1)} %get-tuple-element.138), channel_id=1, source_target_pairs={{0,32},{32,64},{64,96},{96,128},{128,160},{160,192},{192,224},{1,3... | collective-permute-start | bytes 73736 | tf_op jit(solution)/shard_map/ppermute | solution.py:33
  185.6 4.6 %collective-permute-start.17 = (f32[3,8,1,256]{3,2,1,0:T(1,128)S(1)}, f32[3,8,1,256]{3,2,1,0:T(1,128)S(1)}, u32[]{:S(2)}, u32[]{:S(2)}) collective-permute-start(f32[3,8,1,256]{3,2,1,0:T(1,128)S(1)} %get-tuple-element.139), channel_id=1, source_target_pairs={{32,0},{64,32},{96,64},{128,96},{160,128},{192,160},{224,192},{33,... | collective-permute-start | bytes 73736 | tf_op jit(solution)/shard_map/ppermute | solution.py:34
  190.4 8.8 %collective-permute-start.18 = (f32[3,8,18,1]{3,2,1,0:T(8,128)S(1)}, f32[3,8,18,1]{3,2,1,0:T(8,128)S(1)}, u32[]{:S(2)}, u32[]{:S(2)}) collective-permute-start(f32[3,8,18,1]{3,2,1,0:T(8,128)S(1)} %get-tuple-element.128), channel_id=1, source_target_pairs={{0,2},{2,4},{4,6},{6,8},{8,10},{10,12},{12,14},{14,16},{16,18},{18... | collective-permute-start | bytes 5192 | tf_op jit(solution)/shard_map/ppermute | solution.py:33
  195.5 8.0 %collective-permute-start.19 = (f32[3,8,18,1]{3,2,1,0:T(8,128)S(1)}, f32[3,8,18,1]{3,2,1,0:T(8,128)S(1)}, u32[]{:S(2)}, u32[]{:S(2)}) collective-permute-start(f32[3,8,18,1]{3,2,1,0:T(8,128)S(1)} %get-tuple-element.129), channel_id=1, source_target_pairs={{2,0},{4,2},{6,4},{8,6},{10,8},{12,10},{14,12},{16,14},{18,16},{20... | collective-permute-start | bytes 5192 | tf_op jit(solution)/shard_map/ppermute | solution.py:34
  203.8 4.0 %collective-permute-start.20 = (f32[3,1,18,258]{3,2,1,0:T(8,128)S(1)}, f32[3,1,18,258]{3,2,1,0:T(8,128)S(1)}, u32[]{:S(2)}, u32[]{:S(2)}) collective-permute-start(f32[3,1,18,258]{3,2,1,0:T(8,128)S(1)} %get-tuple-element.116), channel_id=1, source_target_pairs={{0,1},{2,3},{4,5},{6,7},{8,9},{10,11},{12,13},{14,15},{16,17},{18,... | collective-permute-start | bytes 167192 | tf_op jit(solution)/shard_map/ppermute | solution.py:33
  206.0 7.0 %collective-permute-start.21 = (f32[3,1,18,258]{3,2,1,0:T(8,128)S(1)}, f32[3,1,18,258]{3,2,1,0:T(8,128)S(1)}, u32[]{:S(2)}, u32[]{:S(2)}) collective-permute-start(f32[3,1,18,258]{3,2,1,0:T(8,128)S(1)} %get-tuple-element.117), channel_id=1, source_target_pairs={{1,0},{3,2},{5,4},{7,6},{9,8},{11,10},{13,12},{15,14},{17,16},{19,... | collective-permute-start | bytes 167192 | tf_op jit(solution)/shard_map/ppermute | solution.py:34
  268.1 5.5 %collective-permute-start.23 = (f32[3,8,1,256]{3,2,1,0:T(1,128)S(1)}, f32[3,8,1,256]{3,2,1,0:T(1,128)S(1)}, u32[]{:S(2)}, u32[]{:S(2)}) collective-permute-start(f32[3,8,1,256]{3,2,1,0:T(1,128)S(1)} %get-tuple-element.137), channel_id=1, source_target_pairs={{32,0},{64,32},{96,64},{128,96},{160,128},{192,160},{224,192},{33,... | collective-permute-start | bytes 73736 | tf_op jit(solution)/shard_map/ppermute | solution.py:34
  273.8 8.6 %collective-permute-start.24 = (f32[3,8,18,1]{3,2,1,0:T(8,128)S(1)}, f32[3,8,18,1]{3,2,1,0:T(8,128)S(1)}, u32[]{:S(2)}, u32[]{:S(2)}) collective-permute-start(f32[3,8,18,1]{3,2,1,0:T(8,128)S(1)} %get-tuple-element.126), channel_id=1, source_target_pairs={{0,2},{2,4},{4,6},{6,8},{8,10},{10,12},{12,14},{14,16},{16,18},{18... | collective-permute-start | bytes 5192 | tf_op jit(solution)/shard_map/ppermute | solution.py:33
  278.8 8.0 %collective-permute-start.25 = (f32[3,8,18,1]{3,2,1,0:T(8,128)S(1)}, f32[3,8,18,1]{3,2,1,0:T(8,128)S(1)}, u32[]{:S(2)}, u32[]{:S(2)}) collective-permute-start(f32[3,8,18,1]{3,2,1,0:T(8,128)S(1)} %get-tuple-element.127), channel_id=1, source_target_pairs={{2,0},{4,2},{6,4},{8,6},{10,8},{12,10},{14,12},{16,14},{18,16},{20... | collective-permute-start | bytes 5192 | tf_op jit(solution)/shard_map/ppermute | solution.py:34
  288.8 7.0 %collective-permute-start.27 = (f32[3,1,18,258]{3,2,1,0:T(8,128)S(1)}, f32[3,1,18,258]{3,2,1,0:T(8,128)S(1)}, u32[]{:S(2)}, u32[]{:S(2)}) collective-permute-start(f32[3,1,18,258]{3,2,1,0:T(8,128)S(1)} %get-tuple-element.115), channel_id=1, source_target_pairs={{1,0},{3,2},{5,4},{7,6},{9,8},{11,10},{13,12},{15,14},{17,16},{19,... | collective-permute-start | bytes 167192 | tf_op jit(solution)/shard_map/ppermute | solution.py:34
  (4 other events, 14.6 us)
where the time goes:
time: 351 us; the launch traced here: 350 us
  blocking collectives  140 us (40%)
  starting transfers between devices  71.6 us (20%)
  waiting for transfers between devices  65 us (19%)
  other arithmetic  52.8 us (15%)
  between operations  11.2 us (3%)
  local copies, waits for them, and re-layouts  9.35 us (3%)
    psum x15, blocking collectives, over_axes(): value = lax.psum(value, axis)  127 us
    ppermute x14, waiting for transfers between devices, padded(): after = lax.ppermute(initial, axis, down)  58.5 us
    ppermute x14, starting transfers between devices, padded(): before = lax.ppermute(last, axis, up)  48.3 us
    ppermute x14, starting transfers between devices, padded(): after = lax.ppermute(initial, axis, down)  23.3 us
    another operation x9, other arithmetic, apply_operator(): return jnp.stack(parts)  19.1 us
    another operation x2, other arithmetic, per_device(): jnp.stack([starting_kelvin, diffusive_coefficient, power, inverse_cap])  16.4 us
    all_to_all x1, blocking collectives, per_device(): lax.all_to_all(fields, 'gz', split_axis=1, concat_axis=3, tiled=True)  12.7 us
  transfers between devices with their start and end apart: 28, of which 20 were waited for; matrix products, arithmetic and copies ran while one was open for 1% of the time, Pallas kernels for 0%

commit v1 on v0

v1 whole, which is shorter than its diff:
```python
import jax
import jax.numpy as jnp
from jax import lax
from jax.experimental import pallas as pl
from jax.experimental.pallas import tpu as pltpu
from jax.sharding import PartitionSpec as P

MESH = pl.DeviceIdType.MESH
F32 = jnp.float32
TIME_STEP = 0.03
TAU = 4.0 / 3.0
SPAN = 6.0
DIAGONAL = 0.5 + 2.5 + 2.5 + 10.0 / 9.0


def plus(value, axis):
    return pltpu.roll(value, value.shape[axis] - 1, axis)


def minus(value, axis):
    return pltpu.roll(value, 1, axis)


def tree(bits, entries):
    while len(entries) > 1:
        mask, bits = bits[0], bits[1:]
        entries = [jnp.where(mask, entries[i + 1], entries[i]) for i in range(0, len(entries), 2)]
    return entries[0]


def lookup(identity, entries):
    bits, width = [], 1
    while width < len(entries):
        bits.append((identity & width) != 0)
        width *= 2
    return tree(bits, entries)


def conduct(own, other):
    return 2.0 * own * other / jnp.maximum(own + other, 0.25)


def stencil(get):
    def both(comp, kind):
        up, down = get(comp, kind, 1), get(comp, kind, -1)
        return up + down, up - down

    z, x, y = 0, 1, 2
    e, p, q = 0, 1, 2
    pz_ez, qz_ez = both(z, e)
    pz_pz, qz_pz = both(z, p)
    pz_ex, qz_ex = both(x, e)
    pz_px, qz_px = both(x, p)
    pz_qx = get(x, q, 1) + get(x, q, -1)
    pz_qy, qz_qy = both(y, q)
    qz_qz = get(z, q, 1) - get(z, q, -1)
    e_z, p_z = get(z, e, 0), get(z, p, 0)
    e_x, p_x = get(x, e, 0), get(x, p, 0)
    p_y = get(y, p, 0)
    eighth, corner, mixed = 0.125, 5.0 / 36.0, 1.0 / 18.0
    parts = []
    parts.append((
        0.25 * (p_z + pz_pz) + 0.75 * pz_ez + eighth * qz_qy,
        0.25 * (e_z + pz_ez) + eighth * p_z + corner * pz_pz + mixed * qz_qy,
        eighth * qz_ex + mixed * qz_px,
    ))
    shared = 0.25 * (p_x + pz_ex)
    parts.append((
        shared + eighth * pz_px,
        0.75 * e_x + shared + corner * pz_px,
        eighth * (get(y, q, 0) + qz_ez) + mixed * (pz_qy + qz_pz),
    ))
    pz_ey = get(y, e, 1) + get(y, e, -1)
    pz_py = get(y, p, 1) + get(y, p, -1)
    parts.append((
        0.75 * p_y + 0.25 * (pz_ey + pz_py) + eighth * qz_qz,
        0.25 * (get(y, e, 0) + p_y) + eighth * pz_ey + corner * pz_py + mixed * qz_qz,
        eighth * get(x, q, 0) + mixed * pz_qx,
    ))
    return [c + plus(a + b, 0) + minus(a - b, 0) for c, a, b in parts]


def scalar_stencils(get):
    e, p, q = 0, 1, 2
    pz_e, qz_e = get(e, 1) + get(e, -1), get(e, 1) - get(e, -1)
    pz_p, qz_p = get(p, 1) + get(p, -1), get(p, 1) - get(p, -1)
    pz_q, qz_q = get(q, 1) + get(q, -1), get(q, 1) - get(q, -1)
    e0, p0, q0 = get(e, 0), get(p, 0), get(q, 0)
    eighth, corner, mixed = 0.125, 5.0 / 36.0, 1.0 / 18.0

    def even(c, a):
        return c + plus(a, 0) + minus(a, 0)

    def odd(b):
        return plus(b, 0) - minus(b, 0)

    return [
        even(0.25 * (p0 + pz_p) + 0.75 * pz_e, 0.25 * (e0 + pz_e) + eighth * p0 + corner * pz_p),
        even(0.25 * (p0 + pz_e) + eighth * pz_p, 0.75 * e0 + 0.25 * (p0 + pz_e) + corner * pz_p),
        even(0.75 * p0 + 0.25 * (pz_e + pz_p), 0.25 * (e0 + p0) + eighth * pz_e + corner * pz_p),
        odd(eighth * qz_e + mixed * qz_p),
        even(eighth * qz_q, mixed * qz_q),
        odd(eighth * q0 + mixed * pz_q),
    ]


def gradient(get):
    e, p, q = 0, 1, 2
    qz_e, qz_p = get(e, 1) - get(e, -1), get(p, 1) - get(p, -1)
    pz_e, pz_p = get(e, 1) + get(e, -1), get(p, 1) + get(p, -1)
    q0, pz_q = get(q, 0), get(q, 1) + get(q, -1)
    sixth = 1.0 / 6.0
    a_z = 0.25 * qz_e + sixth * qz_p
    b_x = 0.5 * get(e, 0) + 0.25 * (get(p, 0) + pz_e) + sixth * pz_p
    a_y = 0.25 * q0 + sixth * pz_q
    return [
        0.5 * qz_e + 0.25 * qz_p + plus(a_z, 0) + minus(a_z, 0),
        plus(b_x, 0) - minus(b_x, 0),
        0.5 * q0 + 0.25 * pz_q + plus(a_y, 0) + minus(a_y, 0),
    ]


def poly_dot(first, second, moments):
    total = None
    for i, a in enumerate(first):
        for j, b in enumerate(second):
            term = a * b * moments[i + j]
            total = term if total is None else total + term
    return total


def shifted(poly):
    out = [TAU * c for c in poly] + [jnp.zeros_like(poly[0])]
    for k, c in enumerate(poly):
        out[k + 1] = out[k + 1] + c
    return out


def added(first, second):
    if len(first) < len(second):
        first, second = second, first
    return [a + second[i] if i < len(second) else a for i, a in enumerate(first)]


def iterate_coefficients(moments):
    one = jnp.ones_like(moments[0])
    residual, direction, solution = [one], [one], []
    norm = moments[0]
    for number in range(3):
        image = shifted(direction)
        alpha = norm / poly_dot(direction, image, moments)
        solution = added(solution, [alpha * c for c in direction])
        residual = added([-alpha * c for c in image], residual)
        if number < 2:
            following = poly_dot(residual, residual, moments)
            ratio = following / norm
            direction = added(residual, [ratio * c for c in direction])
            norm = following
    return solution, residual


def make_kernel(sizes):
    nx, ny = sizes["gx"], sizes["gy"]
    group_a, group_b = nx * 2, ny

    def kernel(
        kelvin_in, label_in, patch_in, traits, intensity,
        warmed_out, solution_out, residual_out,
        temp, label, patch, cond, rate, power, g_row, g_col, g_up, temp_one,
        packs, strips, packed_strain, strain_strips, label_strips,
        strain, e_label, e_strain, base, field, lanes, stiff,
        sums, sums_a, sums_b, total_a,
        local_sem, send, recv,
    ):
        gx, gy, gz = lax.axis_index("gx"), lax.axis_index("gy"), lax.axis_index("gz")
        other = 1 - gz
        nexts = {-1: lax.rem(gx + nx - 1, nx), 0: gx, 1: lax.rem(gx + 1, nx)}
        gy_up, gy_down = lax.rem(gy + 1, ny), lax.rem(gy + ny - 1, ny)
        own_lanes = pl.ds(pl.multiple_of(gz * 128, 128), 128)

        loads = [
            pltpu.make_async_copy(kelvin_in, temp.at[:, 0:16, 0:128], local_sem.at[0]),
            pltpu.make_async_copy(label_in, label.at[:, 0:16, 0:128], local_sem.at[1]),
            pltpu.make_async_copy(patch_in, patch.at[:, 0:16, 0:128], local_sem.at[2]),
            pltpu.make_async_copy(
                label_in.at[pl.ds(4 * gz, 12)], e_label.at[:, 0:16, own_lanes], local_sem.at[3]
            ),
        ]
        for copy in loads:
            copy.start()
        temp[:, 16:24, 0:128] = jnp.zeros((16, 8, 128), F32)
        label[:, 16:24, 0:128] = jnp.zeros((16, 8, 128), jnp.int32)
        patch[:, 16:24, 0:128] = jnp.zeros((16, 8, 128), jnp.int32)

        barrier = pltpu.get_barrier_semaphore()
        peers = [
            (nexts[dx], dy, dz)
            for dx in (-1, 0, 1)
            for dy in (gy, gy_up, gy_down)
            for dz in (gz, other)
            if not (dx == 0 and dy is gy and dz is gz)
        ]
        number_a = gx * 2 + gz
        ring_a = []
        for step in range(1, group_a):
            there = lax.rem(number_a + step, group_a)
            ring_a.append((there // 2, gy, lax.rem(there, 2)))
        ring_b = [(gx, lax.rem(gy + step, ny), gz) for step in range(1, group_b)]
        everyone = peers + ring_a + ring_b
        for peer in everyone:
            pl.semaphore_signal(barrier, inc=1, device_id=peer, device_id_type=MESH)
        for copy in loads:
            copy.wait()

        lane = lax.broadcasted_iota(jnp.int32, (8, 128), 1)
        sub = lax.broadcasted_iota(jnp.int32, (8, 128), 0)

        def pack(read, width, sides):
            def body(layer, acc):
                acc = list(acc)
                for half in range(2):
                    slot = layer * 2 + half
                    mask = (lane >> 2) == slot
                    for k in range(width):
                        value = read(k, layer, half)
                        for n, start in enumerate(sides):
                            moved = pltpu.roll(value, lax.rem(slot * 4 + 128 - start, 128), 1)
                            acc[k * len(sides) + n] = jnp.where(mask, moved, acc[k * len(sides) + n])
                return tuple(acc)

            return lax.fori_loop(0, 16, body, tuple(jnp.zeros((8, 128), F32) for _ in range(width * len(sides))))

        def read_inputs(k, layer, half):
            ref = (temp, label, patch)[k]
            return ref[layer, 8 * half : 8 * half + 8, 0:128].astype(F32)

        packed = pack(read_inputs, 3, (0, 124))
        for k in range(3):
            for side in range(2):
                packs[side, k] = packed[k * 2 + side]

        pl.semaphore_wait(barrier, len(everyone))

        count = [0]

        def remote(src, dst, peer):
            n = count[0]
            count[0] += 1
            copy = pltpu.make_async_remote_copy(
                src_ref=src, dst_ref=dst, send_sem=send.at[n], recv_sem=recv.at[n],
                device_id=peer, device_id_type=MESH,
            )
            copy.start()
            return copy

        heat = []
        for ref in (temp, label, patch):
            heat.append(remote(ref.at[:, 0:2, 0:128], ref.at[:, 16:18, 0:128], (nexts[-1], gy, gz)))
            heat.append(remote(ref.at[:, 14:16, 0:128], ref.at[:, 22:24, 0:128], (nexts[1], gy, gz)))
        right_gy = jnp.where(gz == 0, gy, gy_up)
        left_gy = jnp.where(gz == 0, gy_down, gy)
        for dx in (0, -1, 1):
            heat.append(remote(packs.at[0], strips.at[0, 1 - dx], (nexts[dx], left_gy, other)))
            heat.append(remote(packs.at[1], strips.at[1, 1 - dx], (nexts[dx], right_gy, other)))

        side_gy = jnp.where(gz == 0, gy_down, gy_up)

        def elastic_sends(src, src_layers, dst, pack_src, pack_dst):
            out = [remote(src.at[pl.ds(src_layers(other), 12), 0:16, 0:128], dst.at[:, 0:16, own_lanes], (gx, gy, other))]
            for dz in (gz, other):
                layers = pl.ds(src_layers(dz), 12)
                out.append(remote(src.at[layers, 0:4, 0:128], dst.at[:, 16:20, own_lanes], (nexts[-1], gy, dz)))
                out.append(remote(src.at[layers, 12:16, 0:128], dst.at[:, 20:24, own_lanes], (nexts[1], gy, dz)))
                for dx in (0, -1, 1):
                    out.append(remote(pack_src, pack_dst.at[gz, 1 - dx], (nexts[dx], side_gy, dz)))
            return out

        labels = elastic_sends(label, lambda dz: 4 * dz, e_label, packs.at[gz, 1], label_strips)

        for copy in heat:
            copy.wait_recv()

        def halo_blocks(blocks):
            right = [blocks(0, d) for d in (-1, 0, 1)]
            left = [blocks(1, d) for d in (-1, 0, 1)]

            def corner(three):
                return jnp.where(sub < 4, three[2], pltpu.roll(three[0], 124, 1))

            right_corner, left_corner = corner(right), corner(left)

            def at(layer):
                def one(r, l, slot):
                    r = pltpu.roll(r, lax.rem(128 - slot * 4, 128), 1)
                    l = pltpu.roll(l, lax.rem(252 - slot * 4, 128), 1)
                    return jnp.where(lane < 64, r, l)

                return jnp.concatenate([
                    one(right[1], left[1], layer * 2),
                    one(right[1], left[1], layer * 2 + 1),
                    one(right_corner, left_corner, layer * 2),
                ], axis=0)

            return at

        temp_halo, label_halo, patch_halo = [
            halo_blocks(lambda side, d, k=k: strips[side, d + 1, k]) for k in range(3)
        ]

        row = lax.broadcasted_iota(jnp.int32, (24, 128), 0)
        wide_lane = lax.broadcasted_iota(jnp.int32, (24, 128), 1)
        low_row = jnp.where(gx == nx - 1, 16, 24)
        high_row = jnp.where(gx == 0, 20, 32)
        rows_ok = ((row < 16) | ((row >= 16) & (row < 20) & (row < low_row)) | ((row >= 20) & (row < high_row) & (gx > 0)))
        first_tile, last_tile = (gy == 0) & (gz == 0), (gy == ny - 1) & (gz == 1)
        right_limit = jnp.where(last_tile, 0, 64)
        left_limit = jnp.where(first_tile, 128, 64)
        cols_ok = (wide_lane < right_limit) | (wide_lane >= left_limit)
        grid_ok = [rows_ok, rows_ok & cols_ok]
        e_right_limit = jnp.where(gy == ny - 1, 0, 64)
        e_left_limit = jnp.where(gy == 0, 128, 64)
        e_cols_ok = (wide_lane < e_right_limit) | (wide_lane >= e_left_limit)
        e_ok = [rows_ok, rows_ok, rows_ok & e_cols_ok]

        materials = range(4)
        conductivity = [traits[0, m] for m in materials]
        capacity = [traits[1, m] for m in materials]
        modulus = [traits[2, m] for m in materials]
        expansion = [traits[3, m] for m in materials]
        tiles = [intensity[t] for t in range(16)]

        def heat_fields(layer, carry):
            temp[layer, :, 128:256] = temp_halo(layer)
            ids = [label[layer, :, 0:128], label_halo(layer).astype(jnp.int32)]
            tile_ids = [patch[layer, :, 0:128], patch_halo(layer).astype(jnp.int32)]
            for n in range(2):
                cut = slice(128 * n, 128 * n + 128)
                cond[layer, :, cut] = jnp.where(grid_ok[n], lookup(ids[n], conductivity), 0.0)
                rate[layer, :, cut] = TIME_STEP / lookup(ids[n], capacity)
                power[layer, :, cut] = lookup(tile_ids[n], tiles)
            return carry

        lax.fori_loop(0, 16, heat_fields, 0)
        cond[16] = jnp.zeros((24, 256), F32)

        def conductances(layer, carry):
            own = cond[layer]
            g_row[layer] = conduct(own, plus(own, 0))
            g_col[layer] = conduct(own, plus(own, 1))
            g_up[layer + 1] = conduct(own, cond[layer + 1])
            return carry

        g_up[0] = jnp.zeros((24, 256), F32)
        lax.fori_loop(0, 16, conductances, 0)

        def heat_step(source, layer):
            own = source[layer]
            above, below = source[jnp.minimum(layer + 1, 15)], source[jnp.maximum(layer - 1, 0)]
            row_flux = g_row[layer] * (plus(own, 0) - own)
            col_flux = g_col[layer] * (plus(own, 1) - own)
            flux = row_flux - minus(row_flux, 0) + col_flux - minus(col_flux, 1)
            flux = flux + g_up[layer + 1] * (above - own) + g_up[layer] * (below - own)
            return own + rate[layer] * (flux + power[layer])

        def heat_one(layer, carry):
            temp_one[layer] = heat_step(temp, layer)
            return carry

        lax.fori_loop(0, 16, heat_one, 0)

        def heat_two(layer, carry):
            warm = heat_step(temp_one, layer)[0:16, 0:128]
            warmed_out[layer] = warm
            strain[layer] = lookup(label[layer, 0:16, 0:128], expansion) * warm
            return carry

        lax.fori_loop(0, 16, heat_two, 0)

        start = jnp.where(gz == 0, 0, 124)

        def pack_strain(layer, acc):
            for half in range(2):
                slot = layer * 2 + half
                moved = pltpu.roll(strain[layer, 8 * half : 8 * half + 8], lax.rem(slot * 4 + 128 - start, 128), 1)
                acc = jnp.where((lane >> 2) == slot, moved, acc)
            return acc

        packed_strain[...] = lax.fori_loop(0, 16, pack_strain, jnp.zeros((8, 128), F32))
        strains = elastic_sends(strain, lambda dz: 4 * dz, e_strain, packed_strain, strain_strips)

        def own_strain(layer, carry):
            e_strain[layer, 0:16, own_lanes] = strain[layer + 4 * gz]
            return carry

        lax.fori_loop(0, 12, own_strain, 0)

        for ref in (base, field, lanes):
            for n in range(ref.shape[0]):
                for m in range(ref.shape[1]):
                    ref[n, m, 0] = jnp.zeros((24, 384), F32)

        largest = jnp.maximum(jnp.maximum(modulus[0], modulus[1]), jnp.maximum(modulus[2], modulus[3]))
        scale = SPAN * largest
        inverse = 1.0 / jnp.full((1, 128), scale, F32)
        scaled = [m * inverse for m in modulus]

        for copy in labels:
            copy.wait_recv()
        for copy in strains:
            copy.wait_recv()

        e_label_halo = halo_blocks(lambda side, d: label_strips[side, d + 1])
        e_strain_halo = halo_blocks(lambda side, d: strain_strips[side, d + 1])

        def stacked(layer):
            return jnp.where(gz == 0, layer, 11 - layer)

        def spread(ref, n, layer, value):
            ahead, behind = plus(value, 1), minus(value, 1)
            ref[n, 0, layer + 1] = value
            ref[n, 1, layer + 1] = ahead + behind
            ref[n, 2, layer + 1] = ahead - behind

        def base_fields(layer, carry):
            raw = stacked(layer)
            ids = [e_label[raw, :, 0:128], e_label[raw, :, 128:256]]
            hot = [e_strain[raw, :, 0:128], e_strain[raw, :, 128:256]]
            whole = raw + 4 * gz
            ids.append(e_label_halo(whole).astype(jnp.int32))
            hot.append(e_strain_halo(whole))
            stiffness = [jnp.where(e_ok[n], lookup(ids[n], scaled), 0.0) for n in range(3)]
            hot = [jnp.where(e_ok[n], hot[n], 0.0) for n in range(3)]
            e = jnp.concatenate(stiffness, axis=1)
            s = jnp.concatenate(hot, axis=1)
            spread(base, 0, layer, e)
            spread(base, 1, layer, s)
            spread(base, 2, layer, e * s)
            return carry

        lax.fori_loop(0, 12, base_fields, 0)

        cuts = [slice(128 * n, 128 * n + 128) for n in range(3)]

        def put(step, layer, chunks):
            e = base[0, 0, layer + 1]
            for comp in range(3):
                value = jnp.concatenate(chunks[comp], axis=1)
                field[step, comp, layer + 1] = value
                if step < 3:
                    ahead, behind = plus(value, 1), minus(value, 1)
                    slot = (step % 2) * 5
                    lanes[slot, comp, layer + 1] = ahead + behind
                    lanes[slot + 1, comp, layer + 1] = ahead - behind
                    value = e * value
                    ahead, behind = plus(value, 1), minus(value, 1)
                    lanes[slot + 2, comp, layer + 1] = value
                    lanes[slot + 3, comp, layer + 1] = ahead + behind
                    lanes[slot + 4, comp, layer + 1] = ahead - behind

        def first_vector(layer, carry):
            chunks = [[], [], []]
            for cut in cuts:
                def get(n):
                    return lambda kind, dz: base[n, kind, layer + 1 + dz, :, cut]

                e, s = base[0, 0, layer + 1, :, cut], base[1, 0, layer + 1, :, cut]
                inside = e > 0.0
                de, ds, des = gradient(get(0)), gradient(get(1)), gradient(get(2))
                for comp in range(3):
                    load = -(e * ds[comp] + s * de[comp] + des[comp])
                    chunks[comp].append(jnp.where(inside, load, 0.0))
                for n, value in enumerate(scalar_stencils(get(0))):
                    stiff[n, layer, :, cut] = value
            put(0, layer, chunks)
            return carry

        lax.fori_loop(0, 11, first_vector, 0)

        def next_vector(step, layer):
            chunks = [[], [], []]
            slot = (step % 2) * 5
            for cut in cuts:
                def plain(comp, kind, dz):
                    if kind == 0:
                        return field[step, comp, layer + 1 + dz, :, cut]
                    return lanes[slot + kind - 1, comp, layer + 1 + dz, :, cut]

                def weighted(comp, kind, dz):
                    return lanes[slot + 2 + kind, comp, layer + 1 + dz, :, cut]

                ku, kw = stencil(plain), stencil(weighted)
                e = base[0, 0, layer + 1, :, cut]
                inside = e > 0.0
                zz, xx, yy, zx, zy, xy = [stiff[n, layer, :, cut] for n in range(6)]
                u = [plain(comp, 0, 0) for comp in range(3)]
                gu = [
                    zz * u[0] + zx * u[1] + zy * u[2],
                    zx * u[0] + xx * u[1] + xy * u[2],
                    zy * u[0] + xy * u[1] + yy * u[2],
                ]
                for comp in range(3):
                    value = e * (DIAGONAL * u[comp] - ku[comp]) + gu[comp] - kw[comp] - TAU * u[comp]
                    chunks[comp].append(jnp.where(inside, value, 0.0))
            put(step + 1, layer, chunks)

        for step in range(3):
            def body(layer, carry, step=step):
                next_vector(step, layer)
                return carry

            lax.fori_loop(0, 10 - step, body, 0)

        def products(layer, acc):
            acc = list(acc)
            for comp in range(3):
                for half in range(2):
                    for n in range(2):
                        v = [
                            field[step, comp, layer + 1, 8 * half : 8 * half + 8, 128 * n : 128 * n + 128]
                            for step in range(4)
                        ]
                        for k in range(6):
                            acc[k] = acc[k] + v[k // 2] * v[k - k // 2]
            return tuple(acc)

        acc = lax.fori_loop(0, 8, products, tuple(jnp.zeros((8, 128), F32) for _ in range(6)))
        mine = jnp.zeros((8, 128), F32)
        for k in range(6):
            mine = jnp.where(sub == k, jnp.sum(acc[k], axis=0, keepdims=True), mine)
        sums[...] = mine

        def reduce_over(ring, src, dst):
            copies = [remote(src, dst.at[n], peer) for n, peer in enumerate(ring)]
            for copy in copies:
                copy.wait_recv()
            value = src[...]
            for n in range(len(ring)):
                value = value + dst[n]
            return copies, value

        first, value = reduce_over(ring_a, sums, sums_a)
        total_a[...] = value
        second, value = reduce_over(ring_b, total_a, sums_b)

        total = jnp.sum(value, axis=1, keepdims=True)
        moments = [total[k : k + 1] for k in range(6)]
        x_of, r_of = iterate_coefficients(moments)
        x_of = [jnp.broadcast_to(c, (16, 256)) for c in x_of]
        r_of = [jnp.broadcast_to(c * scale, (16, 256)) for c in r_of]
        sign = jnp.where(gz == 0, 1.0, -1.0)

        def outputs(layer, carry):
            place = jnp.where(gz == 0, layer, 7 - layer)
            for comp in range(3):
                v = [field[step, comp, layer + 1, 0:16, 0:256] for step in range(4)]
                x = x_of[0] * v[0] + x_of[1] * v[1] + x_of[2] * v[2]
                r = r_of[0] * v[0] + r_of[1] * v[1] + r_of[2] * v[2] + r_of[3] * v[3]
                solution_out[comp, place] = x * sign if comp == 0 else x
                residual_out[comp, place] = r * sign if comp == 0 else r
            return carry

        lax.fori_loop(0, 8, outputs, 0)

        for copy in heat + labels + strains + first + second:
            copy.wait_send()

    return kernel


def solution(mesh):
    sizes = dict(mesh.shape)
    copies = 12 + 11 + 11 + (2 * sizes["gx"] - 1) + (sizes["gy"] - 1)

    def per_device(kelvin, label, patch, traits, intensity):
        hbm = pl.BlockSpec(memory_space=pltpu.HBM)
        smem = pl.BlockSpec(memory_space=pltpu.SMEM)
        vmem = pl.BlockSpec(memory_space=pltpu.VMEM)
        heat = lambda layers=16, kind=F32: pltpu.VMEM((layers, 24, 256), kind)
        block = lambda *lead: pltpu.VMEM((*lead, 8, 128), F32)
        wide = lambda *lead: pltpu.VMEM((*lead, 24, 384), F32)
        return pl.pallas_call(
            make_kernel(sizes),
            out_shape=(
                jax.ShapeDtypeStruct((16, 16, 128), F32),
                jax.ShapeDtypeStruct((3, 8, 16, 256), F32),
                jax.ShapeDtypeStruct((3, 8, 16, 256), F32),
            ),
            in_specs=[hbm, hbm, hbm, smem, smem],
            out_specs=(vmem, vmem, vmem),
            scratch_shapes=[
                heat(), heat(kind=jnp.int32), heat(kind=jnp.int32),
                heat(17), heat(), heat(), heat(), heat(), heat(17), heat(),
                block(2, 3), block(2, 3, 3), block(), block(2, 3), block(2, 3),
                pltpu.VMEM((16, 16, 128), F32),
                pltpu.VMEM((12, 24, 384), jnp.int32), wide(12),
                wide(3, 3, 13), wide(4, 3, 13), wide(10, 3, 13), wide(6, 11),
                block(), block(2 * sizes["gx"] - 1), block(sizes["gy"] - 1), block(),
                pltpu.SemaphoreType.DMA((4,)),
                pltpu.SemaphoreType.DMA((copies,)),
                pltpu.SemaphoreType.DMA((copies,)),
            ],
            compiler_params=pltpu.CompilerParams(
                collective_id=0, has_side_effects=True, vmem_limit_bytes=60 * 1024 * 1024
            ),
        )(kelvin, label, patch, traits, intensity)

    columns = P(None, "gx", ("gy", "gz"))
    return jax.shard_map(
        per_device,
        mesh=mesh,
        in_specs=(columns, columns, columns, P(), P()),
        out_specs=(columns, P(None, "gz", "gx", "gy"), P(None, "gz", "gx", "gy")),
        check_vma=False,
    )
```

time: 351 us -> 66.6 us (0.19)
  blocking collectives: 140 us -> 0 us
  starting transfers between devices: 71.6 us -> 0 us
  waiting for transfers between devices: 65 us -> 0 us
  Pallas kernels: 0 us -> 61.6 us
  other arithmetic: 52.8 us -> 0 us
  between operations: 11.2 us -> 0.64 us
  local copies, waits for them, and re-layouts: 9.35 us -> 4.13 us
    psum x15 -> x0, blocking collectives: 127 us -> none  [over_axes(): value = lax.psum(value, axis)]
    ppermute x28 -> x0, starting transfers between devices: 71.6 us -> none  [the longest x14 48.3 us: padded(): before = lax.ppermute(last, axis, up)]
    ppermute x28 -> x0, waiting for transfers between devices: 65 us -> none  [the longest x14 58.5 us: padded(): after = lax.ppermute(initial, axis, down)]
    pallas_call x0 -> x1, Pallas kernels: none -> 61.6 us  [per_device(): pl.pallas_call(make_kernel(sizes), out_shape=(jax.ShapeDtypeStruct((16, 1...]
    another operation x15 -> x0, other arithmetic: 42 us -> none  [the longest x9 19.1 us: apply_operator(): return jnp.stack(parts)]
    all_to_all x1 -> x0, blocking collectives: 12.7 us -> none  [per_device(): lax.all_to_all(fields, 'gz', split_axis=1, concat_axis=3, tiled=True)]
    slice x20 -> x0, local copies, waits for them, and re-layouts: 6.5 us -> none  [the longest x2 3.93 us: lookup(): table[number]]
    sub x6 -> x0, other arithmetic: 3.84 us -> none  [the longest x3 2.52 us: thermal_load(): parts[index_c] = parts[index_c] - strain_gain * direction_part * pushing]
  transfers between devices with their start and end apart: 28 -> 0, of which waited for: 20 -> 0; matrix products, arithmetic and copies ran while one was open for 1% -> 0% of each run, Pallas kernels for 0% -> 0%
where the time goes in v1:
time: 66.6 us; the launch traced here: 66.4 us
  Pallas kernels  61.6 us (92%)
  local copies, waits for them, and re-layouts  4.13 us (6%)
    pallas_call x1, Pallas kernels, per_device(): pl.pallas_call(make_kernel(sizes), out_shape=(jax.ShapeDtypeStruct((16, 1...  61.6 us
    unnamed x5, local copies, waits for them, and re-layouts  4.13 us

profile of v1, /device:TPU:1, one launch (start us, length us, event | category | flops | bytes accessed | tf_op | source)
XLA Modules:
  0.0 66.4 jit_solution(15341578547849259841)
XLA Ops:
  0.6 61.6 %shard_map.76 = (f32[16,16,128]{2,1,0:T(8,128)}, f32[3,8,16,256]{3,2,1,0:T(8,128)}, f32[3,8,16,256]{3,2,1,0:T(8,128)}) custom-call(f32[16,16,128]{2,1,0:T(8,128)} %kelvin_in.1, s32[16,16,128]{2,1,0:T(8,128)} %label_in.1, s32[16,16,128]{2,1,0:T(8,128)} %patch_in.1, f32[4,4]{1,0:T(4,128)} %traits.1, f32[16]{0:T(128)} %intensity.1), custom_call_target="tpu_custom_call" | custom-call | tf_op jit(solution)/shard_map/pallas_call | solution.py:581
  62.3 1.6 %copy.11 = f32[16,16,128]{2,1,0:T(8,128)} copy(f32[16,16,128]{2,1,0:T(8,128)} %get-tuple-element.6) | data formatting | bytes 262144
  63.8 0.0 copy-start
  63.8 1.8 %copy.12 = f32[3,8,16,256]{3,2,1,0:T(8,128)} copy(f32[3,8,16,256]{3,2,1,0:T(8,128)} %get-tuple-element.7) | data formatting | bytes 786432
  65.7 0.0 copy-done
  65.7 0.7 %copy.13 = f32[3,8,16,256]{3,2,1,0:T(8,128)} copy(f32[3,8,16,256]{3,2,1,0:T(8,128)S(1)} %copy-done) | data formatting | bytes 786432
Async XLA Ops:
  63.8 1.8 %copy-start = (f32[3,8,16,256]{3,2,1,0:T(8,128)S(1)}, f32[3,8,16,256]{3,2,1,0:T(8,128)}, u32[]{:S(2)}) copy-start(f32[3,8,16,256]{3,2,1,0:T(8,128)} %get-tuple-element.8) | copy-start | bytes 1179652

commit v2 on v1

--- a/solution.py
+++ b/solution.py
@@ -159,6 +159,15 @@
     return solution, residual
 
 
+def grouped(total, size, body, init):
+    def trip(number, carry):
+        for k in range(size):
+            carry = body(number * size + k, carry)
+        return carry
+
+    return lax.fori_loop(0, total // size, trip, init)
+
+
 def make_kernel(sizes):
     nx, ny = sizes["gx"], sizes["gy"]
     group_a, group_b = nx * 2, ny
@@ -166,7 +175,7 @@
     def kernel(
         kelvin_in, label_in, patch_in, traits, intensity,
         warmed_out, solution_out, residual_out,
-        temp, label, patch, cond, rate, power, g_row, g_col, g_up, temp_one,
+        temp, label, patch, cond, rate, power, g_row, g_row_back, g_col, g_col_back, g_up, temp_one,
         packs, strips, packed_strain, strain_strips, label_strips,
         strain, e_label, e_strain, base, field, lanes, stiff,
         sums, sums_a, sums_b, total_a,
@@ -191,6 +200,9 @@
         temp[:, 16:24, 0:128] = jnp.zeros((16, 8, 128), F32)
         label[:, 16:24, 0:128] = jnp.zeros((16, 8, 128), jnp.int32)
         patch[:, 16:24, 0:128] = jnp.zeros((16, 8, 128), jnp.int32)
+        for side in range(2):
+            for d in (0, 2):
+                strips[side, d] = jnp.zeros((2, 8, 128), F32)
 
         barrier = pltpu.get_barrier_semaphore()
         peers = [
@@ -206,7 +218,7 @@
             there = lax.rem(number_a + step, group_a)
             ring_a.append((there // 2, gy, lax.rem(there, 2)))
         ring_b = [(gx, lax.rem(gy + step, ny), gz) for step in range(1, group_b)]
-        everyone = peers + ring_a + ring_b
+        everyone = peers + ring_a[2:-2] + ring_b[1:-1] if nx > 2 and ny > 2 else peers + ring_a + ring_b
         for peer in everyone:
             pl.semaphore_signal(barrier, inc=1, device_id=peer, device_id_type=MESH)
         for copy in loads:
@@ -215,29 +227,27 @@
         lane = lax.broadcasted_iota(jnp.int32, (8, 128), 1)
         sub = lax.broadcasted_iota(jnp.int32, (8, 128), 0)
 
-        def pack(read, width, sides):
-            def body(layer, acc):
-                acc = list(acc)
-                for half in range(2):
-                    slot = layer * 2 + half
-                    mask = (lane >> 2) == slot
-                    for k in range(width):
-                        value = read(k, layer, half)
-                        for n, start in enumerate(sides):
-                            moved = pltpu.roll(value, lax.rem(slot * 4 + 128 - start, 128), 1)
-                            acc[k * len(sides) + n] = jnp.where(mask, moved, acc[k * len(sides) + n])
-                return tuple(acc)
-
-            return lax.fori_loop(0, 16, body, tuple(jnp.zeros((8, 128), F32) for _ in range(width * len(sides))))
-
-        def read_inputs(k, layer, half):
-            ref = (temp, label, patch)[k]
-            return ref[layer, 8 * half : 8 * half + 8, 0:128].astype(F32)
-
-        packed = pack(read_inputs, 3, (0, 124))
-        for k in range(3):
-            for side in range(2):
-                packs[side, k] = packed[k * 2 + side]
+        def pack_inputs(layer, acc):
+            acc = list(acc)
+            for half in range(2):
+                slot = layer * 2 + half
+                rows = slice(8 * half, 8 * half + 8)
+                place = lane - slot * 4
+                ids = label[layer, rows, 0:128].astype(F32)
+                kelvin = temp[layer, rows, 0:128]
+                tile_ids = patch[layer, rows, 0:128].astype(F32)
+                for side, (four, two) in enumerate(((0, 0), (124, 126))):
+                    moved = pltpu.roll(ids, lax.rem(slot * 4 + 128 - four, 128), 1)
+                    acc[2 * side] = jnp.where((lane >> 2) == slot, moved, acc[2 * side])
+                    moved = pltpu.roll(kelvin, lax.rem(slot * 4 + 128 - two, 128), 1)
+                    acc[2 * side + 1] = jnp.where((place >= 0) & (place < 2), moved, acc[2 * side + 1])
+                    moved = pltpu.roll(tile_ids, lax.rem(slot * 4 + 130 - two, 128), 1)
+                    acc[2 * side + 1] = jnp.where((place >= 2) & (place < 4), moved, acc[2 * side + 1])
+            return tuple(acc)
+
+        packed = grouped(16, 8, pack_inputs, tuple(jnp.zeros((8, 128), F32) for _ in range(4)))
+        for k in range(4):
+            packs[k // 2, k % 2] = packed[k]
 
         pl.semaphore_wait(barrier, len(everyone))
 
@@ -254,14 +264,16 @@
             return copy
 
         heat = []
-        for ref in (temp, label, patch):
-            heat.append(remote(ref.at[:, 0:2, 0:128], ref.at[:, 16:18, 0:128], (nexts[-1], gy, gz)))
-            heat.append(remote(ref.at[:, 14:16, 0:128], ref.at[:, 22:24, 0:128], (nexts[1], gy, gz)))
+        for ref, deep in ((temp, 2), (label, 2), (patch, 1)):
+            up, down = slice(16 - deep, 16), slice(24 - deep, 24)
+            heat.append(remote(ref.at[:, 0:deep, 0:128], ref.at[:, 16 : 16 + deep, 0:128], (nexts[-1], gy, gz)))
+            heat.append(remote(ref.at[:, up, 0:128], ref.at[:, down, 0:128], (nexts[1], gy, gz)))
         right_gy = jnp.where(gz == 0, gy, gy_up)
         left_gy = jnp.where(gz == 0, gy_down, gy)
         for dx in (0, -1, 1):
-            heat.append(remote(packs.at[0], strips.at[0, 1 - dx], (nexts[dx], left_gy, other)))
-            heat.append(remote(packs.at[1], strips.at[1, 1 - dx], (nexts[dx], right_gy, other)))
+            rows = {0: slice(0, 8), -1: slice(0, 2), 1: slice(6, 8)}[dx]
+            for side, there in ((0, left_gy), (1, right_gy)):
+                heat.append(remote(packs.at[side, :, rows], strips.at[side, 1 - dx, :, rows], (nexts[dx], there, other)))
 
         side_gy = jnp.where(gz == 0, gy_down, gy_up)
 
@@ -275,12 +287,12 @@
                     out.append(remote(pack_src, pack_dst.at[gz, 1 - dx], (nexts[dx], side_gy, dz)))
             return out
 
-        labels = elastic_sends(label, lambda dz: 4 * dz, e_label, packs.at[gz, 1], label_strips)
-
         for copy in heat:
             copy.wait_recv()
 
-        def halo_blocks(blocks):
+        labels = elastic_sends(label, lambda dz: 4 * dz, e_label, packs.at[gz, 0], label_strips)
+
+        def halo_blocks(blocks, inset=0, last=252):
             right = [blocks(0, d) for d in (-1, 0, 1)]
             left = [blocks(1, d) for d in (-1, 0, 1)]
 
@@ -291,8 +303,8 @@
 
             def at(layer):
                 def one(r, l, slot):
-                    r = pltpu.roll(r, lax.rem(128 - slot * 4, 128), 1)
-                    l = pltpu.roll(l, lax.rem(252 - slot * 4, 128), 1)
+                    r = pltpu.roll(r, lax.rem(256 - inset - slot * 4, 128), 1)
+                    l = pltpu.roll(l, lax.rem(last - inset - slot * 4, 128), 1)
                     return jnp.where(lane < 64, r, l)
 
                 return jnp.concatenate([
@@ -303,9 +315,9 @@
 
             return at
 
-        temp_halo, label_halo, patch_halo = [
-            halo_blocks(lambda side, d, k=k: strips[side, d + 1, k]) for k in range(3)
-        ]
+        label_halo = halo_blocks(lambda side, d: strips[side, d + 1, 0])
+        temp_halo = halo_blocks(lambda side, d: strips[side, d + 1, 1], 0, 254)
+        patch_halo = halo_blocks(lambda side, d: strips[side, d + 1, 1], 2, 254)
 
         row = lax.broadcasted_iota(jnp.int32, (24, 128), 0)
         wide_lane = lax.broadcasted_iota(jnp.int32, (24, 128), 1)
@@ -340,25 +352,25 @@
                 power[layer, :, cut] = lookup(tile_ids[n], tiles)
             return carry
 
-        lax.fori_loop(0, 16, heat_fields, 0)
+        grouped(16, 4, heat_fields, 0)
         cond[16] = jnp.zeros((24, 256), F32)
 
         def conductances(layer, carry):
             own = cond[layer]
-            g_row[layer] = conduct(own, plus(own, 0))
-            g_col[layer] = conduct(own, plus(own, 1))
+            row_g, col_g = conduct(own, plus(own, 0)), conduct(own, plus(own, 1))
+            g_row[layer], g_col[layer] = row_g, col_g
+            g_row_back[layer], g_col_back[layer] = minus(row_g, 0), minus(col_g, 1)
             g_up[layer + 1] = conduct(own, cond[layer + 1])
             return carry
 
         g_up[0] = jnp.zeros((24, 256), F32)
-        lax.fori_loop(0, 16, conductances, 0)
+        grouped(16, 4, conductances, 0)
 
         def heat_step(source, layer):
             own = source[layer]
             above, below = source[jnp.minimum(layer + 1, 15)], source[jnp.maximum(layer - 1, 0)]
-            row_flux = g_row[layer] * (plus(own, 0) - own)
-            col_flux = g_col[layer] * (plus(own, 1) - own)
-            flux = row_flux - minus(row_flux, 0) + col_flux - minus(col_flux, 1)
+            flux = g_row[layer] * (plus(own, 0) - own) + g_row_back[layer] * (minus(own, 0) - own)
+            flux = flux + g_col[layer] * (plus(own, 1) - own) + g_col_back[layer] * (minus(own, 1) - own)
             flux = flux + g_up[layer + 1] * (above - own) + g_up[layer] * (below - own)
             return own + rate[layer] * (flux + power[layer])
 
@@ -366,26 +378,22 @@
             temp_one[layer] = heat_step(temp, layer)
             return carry
 
-        lax.fori_loop(0, 16, heat_one, 0)
-
-        def heat_two(layer, carry):
+        grouped(16, 4, heat_one, 0)
+
+        start = jnp.where(gz == 0, 0, 124)
+
+        def heat_two(layer, acc):
             warm = heat_step(temp_one, layer)[0:16, 0:128]
             warmed_out[layer] = warm
-            strain[layer] = lookup(label[layer, 0:16, 0:128], expansion) * warm
-            return carry
-
-        lax.fori_loop(0, 16, heat_two, 0)
-
-        start = jnp.where(gz == 0, 0, 124)
-
-        def pack_strain(layer, acc):
+            value = lookup(label[layer, 0:16, 0:128], expansion) * warm
+            strain[layer] = value
             for half in range(2):
                 slot = layer * 2 + half
-                moved = pltpu.roll(strain[layer, 8 * half : 8 * half + 8], lax.rem(slot * 4 + 128 - start, 128), 1)
+                moved = pltpu.roll(value[8 * half : 8 * half + 8], lax.rem(slot * 4 + 128 - start, 128), 1)
                 acc = jnp.where((lane >> 2) == slot, moved, acc)
             return acc
 
-        packed_strain[...] = lax.fori_loop(0, 16, pack_strain, jnp.zeros((8, 128), F32))
+        packed_strain[...] = grouped(16, 4, heat_two, jnp.zeros((8, 128), F32))
         strains = elastic_sends(strain, lambda dz: 4 * dz, e_strain, packed_strain, strain_strips)
 
         def own_strain(layer, carry):
@@ -437,7 +445,7 @@
             spread(base, 2, layer, e * s)
             return carry
 
-        lax.fori_loop(0, 12, base_fields, 0)
+        grouped(12, 2, base_fields, 0)
 
         cuts = [slice(128 * n, 128 * n + 128) for n in range(3)]
 
@@ -445,8 +453,10 @@
             e = base[0, 0, layer + 1]
             for comp in range(3):
                 value = jnp.concatenate(chunks[comp], axis=1)
-                field[step, comp, layer + 1] = value
-                if step < 3:
+                if step == 3:
+                    field[step, comp, layer + 1, 0:16, 0:256] = value[0:16]
+                else:
+                    field[step, comp, layer + 1] = value
                     ahead, behind = plus(value, 1), minus(value, 1)
                     slot = (step % 2) * 5
                     lanes[slot, comp, layer + 1] = ahead + behind
@@ -479,7 +489,7 @@
         def next_vector(step, layer):
             chunks = [[], [], []]
             slot = (step % 2) * 5
-            for cut in cuts:
+            for cut in cuts if step < 2 else cuts[:2]:
                 def plain(comp, kind, dz):
                     if kind == 0:
                         return field[step, comp, layer + 1 + dz, :, cut]
@@ -527,7 +537,8 @@
         mine = jnp.zeros((8, 128), F32)
         for k in range(6):
             mine = jnp.where(sub == k, jnp.sum(acc[k], axis=0, keepdims=True), mine)
-        sums[...] = mine
+        mine = jnp.sum(mine, axis=1, keepdims=True)
+        sums[...] = jnp.sum(jnp.where(lane == sub, mine, 0.0), axis=0, keepdims=True)
 
         def reduce_over(ring, src, dst):
             copies = [remote(src, dst.at[n], peer) for n, peer in enumerate(ring)]
@@ -542,8 +553,7 @@
         total_a[...] = value
         second, value = reduce_over(ring_b, total_a, sums_b)
 
-        total = jnp.sum(value, axis=1, keepdims=True)
-        moments = [total[k : k + 1] for k in range(6)]
+        moments = [value[:, k : k + 1] for k in range(6)]
         x_of, r_of = iterate_coefficients(moments)
         x_of = [jnp.broadcast_to(c, (16, 256)) for c in x_of]
         r_of = [jnp.broadcast_to(c * scale, (16, 256)) for c in r_of]
@@ -567,34 +577,45 @@
     return kernel
 
 
+def copy_out(*refs):
+    sems = refs[-1]
+    copies = [pltpu.make_async_copy(refs[n], refs[n + 3], sems.at[n]) for n in range(3)]
+    for copy in copies:
+        copy.start()
+    for copy in copies:
+        copy.wait()
+
+
 def solution(mesh):
     sizes = dict(mesh.shape)
+    hbm = pl.BlockSpec(memory_space=pltpu.HBM)
+    smem = pl.BlockSpec(memory_space=pltpu.SMEM)
+    vmem = pl.BlockSpec(memory_space=pltpu.VMEM)
     copies = 12 + 11 + 11 + (2 * sizes["gx"] - 1) + (sizes["gy"] - 1)
 
     def per_device(kelvin, label, patch, traits, intensity):
-        hbm = pl.BlockSpec(memory_space=pltpu.HBM)
-        smem = pl.BlockSpec(memory_space=pltpu.SMEM)
-        vmem = pl.BlockSpec(memory_space=pltpu.VMEM)
         heat = lambda layers=16, kind=F32: pltpu.VMEM((layers, 24, 256), kind)
         block = lambda *lead: pltpu.VMEM((*lead, 8, 128), F32)
         wide = lambda *lead: pltpu.VMEM((*lead, 24, 384), F32)
-        return pl.pallas_call(
+        row = lambda *lead: pltpu.VMEM((*lead, 1, 128), F32)
+        shapes = (
+            jax.ShapeDtypeStruct((16, 16, 128), F32),
+            jax.ShapeDtypeStruct((3, 8, 16, 256), F32),
+            jax.ShapeDtypeStruct((3, 8, 16, 256), F32),
+        )
+        results = pl.pallas_call(
             make_kernel(sizes),
-            out_shape=(
-                jax.ShapeDtypeStruct((16, 16, 128), F32),
-                jax.ShapeDtypeStruct((3, 8, 16, 256), F32),
-                jax.ShapeDtypeStruct((3, 8, 16, 256), F32),
-            ),
+            out_shape=shapes,
             in_specs=[hbm, hbm, hbm, smem, smem],
             out_specs=(vmem, vmem, vmem),
             scratch_shapes=[
                 heat(), heat(kind=jnp.int32), heat(kind=jnp.int32),
-                heat(17), heat(), heat(), heat(), heat(), heat(17), heat(),
-                block(2, 3), block(2, 3, 3), block(), block(2, 3), block(2, 3),
+                heat(17), heat(), heat(), heat(), heat(), heat(), heat(), heat(17), heat(),
+                block(2, 2), block(2, 3, 2), block(), block(2, 3), block(2, 3),
                 pltpu.VMEM((16, 16, 128), F32),
                 pltpu.VMEM((12, 24, 384), jnp.int32), wide(12),
                 wide(3, 3, 13), wide(4, 3, 13), wide(10, 3, 13), wide(6, 11),
-                block(), block(2 * sizes["gx"] - 1), block(sizes["gy"] - 1), block(),
+                row(), row(2 * sizes["gx"] - 1), row(sizes["gy"] - 1), row(),
                 pltpu.SemaphoreType.DMA((4,)),
                 pltpu.SemaphoreType.DMA((copies,)),
                 pltpu.SemaphoreType.DMA((copies,)),
@@ -603,6 +624,13 @@
                 collective_id=0, has_side_effects=True, vmem_limit_bytes=60 * 1024 * 1024
             ),
         )(kelvin, label, patch, traits, intensity)
+        return pl.pallas_call(
+            copy_out,
+            out_shape=shapes,
+            in_specs=[vmem, vmem, vmem],
+            out_specs=(hbm, hbm, hbm),
+            scratch_shapes=[pltpu.SemaphoreType.DMA((3,))],
+        )(*results)
 
     columns = P(None, "gx", ("gy", "gz"))
     return jax.shard_map(

time: 66.6 us -> 55.4 us (0.83)
  Pallas kernels: 61.6 us -> 54.6 us
  local copies, waits for them, and re-layouts: 4.13 us -> 0 us
    pallas_call x1 -> x2, Pallas kernels: 61.6 us -> 54.6 us  [the longest x1 52.4 us: per_device(): pl.pallas_call(make_kernel(sizes), out_shape=shapes, in_specs=[hbm, hbm,...]
    unnamed x5 -> x0, local copies, waits for them, and re-layouts: 4.13 us -> none
where the time goes in v2:
time: 55.4 us; the launch traced here: 55.2 us
  Pallas kernels  54.6 us (99%)
  between operations  0.64 us (1%)
    pallas_call x1, Pallas kernels, per_device(): pl.pallas_call(make_kernel(sizes), out_shape=shapes, in_specs=[hbm, hbm,...  52.4 us
    pallas_call x1, Pallas kernels, per_device(): pl.pallas_call(copy_out, out_shape=shapes, in_specs=[vmem, vmem, vmem], o...  2.12 us

profile of v2, /device:TPU:1, one launch (start us, length us, event | category | flops | bytes accessed | tf_op | source)
XLA Modules:
  0.0 55.2 jit_solution(8567784581799316741)
XLA Ops:
  0.6 52.4 %shard_map.76 = (f32[16,16,128]{2,1,0:T(8,128)}, f32[3,8,16,256]{3,2,1,0:T(8,128)}, f32[3,8,16,256]{3,2,1,0:T(8,128)}) custom-call(f32[16,16,128]{2,1,0:T(8,128)} %kelvin_in.1, s32[16,16,128]{2,1,0:T(8,128)} %label_in.1, s32[16,16,128]{2,1,0:T(8,128)} %patch_in.1, f32[4,4]{1,0:T(4,128)} %traits.1, f32[16]{0:T(128)} %intensity.1), custom_call_target="tpu_custom_call" | custom-call | tf_op jit(solution)/shard_map/pallas_call | solution.py:606
  53.1 2.1 %shard_map.77 = (f32[16,16,128]{2,1,0:T(8,128)}, f32[3,8,16,256]{3,2,1,0:T(8,128)}, f32[3,8,16,256]{3,2,1,0:T(8,128)}) custom-call(f32[16,16,128]{2,1,0:T(8,128)} %get-tuple-element.6.refs_0_, f32[3,8,16,256]{3,2,1,0:T(8,128)} %get-tuple-element.7.refs_1_, f32[3,8,16,256]{3,2,1,0:T(8,128)} %get-tuple-element.8.refs_2_), custom_call_target="tpu_custom_call" | custom-call | tf_op jit(solution)/shard_map/pallas_call | solution.py:627

commit v3 on v2

--- a/solution.py
+++ b/solution.py
@@ -40,84 +40,75 @@
     return 2.0 * own * other / jnp.maximum(own + other, 0.25)
 
 
-def stencil(get):
-    def both(comp, kind):
-        up, down = get(comp, kind, 1), get(comp, kind, -1)
-        return up + down, up - down
-
-    z, x, y = 0, 1, 2
-    e, p, q = 0, 1, 2
-    pz_ez, qz_ez = both(z, e)
-    pz_pz, qz_pz = both(z, p)
-    pz_ex, qz_ex = both(x, e)
-    pz_px, qz_px = both(x, p)
-    pz_qx = get(x, q, 1) + get(x, q, -1)
-    pz_qy, qz_qy = both(y, q)
-    qz_qz = get(z, q, 1) - get(z, q, -1)
-    e_z, p_z = get(z, e, 0), get(z, p, 0)
-    e_x, p_x = get(x, e, 0), get(x, p, 0)
-    p_y = get(y, p, 0)
-    eighth, corner, mixed = 0.125, 5.0 / 36.0, 1.0 / 18.0
-    parts = []
-    parts.append((
-        0.25 * (p_z + pz_pz) + 0.75 * pz_ez + eighth * qz_qy,
-        0.25 * (e_z + pz_ez) + eighth * p_z + corner * pz_pz + mixed * qz_qy,
-        eighth * qz_ex + mixed * qz_px,
-    ))
-    shared = 0.25 * (p_x + pz_ex)
-    parts.append((
-        shared + eighth * pz_px,
-        0.75 * e_x + shared + corner * pz_px,
-        eighth * (get(y, q, 0) + qz_ez) + mixed * (pz_qy + qz_pz),
-    ))
-    pz_ey = get(y, e, 1) + get(y, e, -1)
-    pz_py = get(y, p, 1) + get(y, p, -1)
-    parts.append((
-        0.75 * p_y + 0.25 * (pz_ey + pz_py) + eighth * qz_qz,
-        0.25 * (get(y, e, 0) + p_y) + eighth * pz_ey + corner * pz_py + mixed * qz_qz,
-        eighth * get(x, q, 0) + mixed * pz_qx,
-    ))
-    return [c + plus(a + b, 0) + minus(a - b, 0) for c, a, b in parts]
+CORNER, MIXED = 10.0 / 9.0, 4.0 / 9.0
+Z, X, Y = 0, 1, 2
+KEPT, SUM, DIFF = 0, 1, 2
+
+
+def even(get, *which):
+    return get(*which, 1) + get(*which, -1)
+
+
+def odd(get, *which):
+    return get(*which, 1) - get(*which, -1)
+
+
+def stencil(get, comp):
+    if comp == Z:
+        e, p = get(Z, KEPT, 0), get(Z, SUM, 0)
+        pe, pp, qq = even(get, Z, KEPT), even(get, Z, SUM), odd(get, Y, DIFF)
+        return (
+            2.0 * (p + pp) + 6.0 * pe + qq,
+            2.0 * (e + pe) + p + CORNER * pp + MIXED * qq,
+            odd(get, X, KEPT) + MIXED * odd(get, X, SUM),
+        )
+    if comp == X:
+        shared = 2.0 * (get(X, SUM, 0) + even(get, X, KEPT))
+        pp = even(get, X, SUM)
+        return (
+            shared + pp,
+            6.0 * get(X, KEPT, 0) + shared + CORNER * pp,
+            get(Y, DIFF, 0) + odd(get, Z, KEPT) + MIXED * (even(get, Y, DIFF) + odd(get, Z, SUM)),
+        )
+    p, pe, pp, qq = get(Y, SUM, 0), even(get, Y, KEPT), even(get, Y, SUM), odd(get, Z, DIFF)
+    return (
+        6.0 * p + 2.0 * (pe + pp) + qq,
+        2.0 * (get(Y, KEPT, 0) + p) + pe + CORNER * pp + MIXED * qq,
+        get(X, DIFF, 0) + MIXED * even(get, X, DIFF),
+    )
 
 
 def scalar_stencils(get):
-    e, p, q = 0, 1, 2
-    pz_e, qz_e = get(e, 1) + get(e, -1), get(e, 1) - get(e, -1)
-    pz_p, qz_p = get(p, 1) + get(p, -1), get(p, 1) - get(p, -1)
-    pz_q, qz_q = get(q, 1) + get(q, -1), get(q, 1) - get(q, -1)
-    e0, p0, q0 = get(e, 0), get(p, 0), get(q, 0)
-    eighth, corner, mixed = 0.125, 5.0 / 36.0, 1.0 / 18.0
-
-    def even(c, a):
+    e, p, q = get(KEPT, 0), get(SUM, 0), get(DIFF, 0)
+    pe, pp, qe, qp = even(get, KEPT), even(get, SUM), odd(get, KEPT), odd(get, SUM)
+    pq, qq = even(get, DIFF), odd(get, DIFF)
+
+    def evenly(c, a):
         return c + plus(a, 0) + minus(a, 0)
 
-    def odd(b):
+    def oddly(b):
         return plus(b, 0) - minus(b, 0)
 
-    return [
-        even(0.25 * (p0 + pz_p) + 0.75 * pz_e, 0.25 * (e0 + pz_e) + eighth * p0 + corner * pz_p),
-        even(0.25 * (p0 + pz_e) + eighth * pz_p, 0.75 * e0 + 0.25 * (p0 + pz_e) + corner * pz_p),
-        even(0.75 * p0 + 0.25 * (pz_e + pz_p), 0.25 * (e0 + p0) + eighth * pz_e + corner * pz_p),
-        odd(eighth * qz_e + mixed * qz_p),
-        even(eighth * qz_q, mixed * qz_q),
-        odd(eighth * q0 + mixed * pz_q),
-    ]
-
-
-def gradient(get):
-    e, p, q = 0, 1, 2
-    qz_e, qz_p = get(e, 1) - get(e, -1), get(p, 1) - get(p, -1)
-    pz_e, pz_p = get(e, 1) + get(e, -1), get(p, 1) + get(p, -1)
-    q0, pz_q = get(q, 0), get(q, 1) + get(q, -1)
-    sixth = 1.0 / 6.0
-    a_z = 0.25 * qz_e + sixth * qz_p
-    b_x = 0.5 * get(e, 0) + 0.25 * (get(p, 0) + pz_e) + sixth * pz_p
-    a_y = 0.25 * q0 + sixth * pz_q
-    return [
-        0.5 * qz_e + 0.25 * qz_p + plus(a_z, 0) + minus(a_z, 0),
-        plus(b_x, 0) - minus(b_x, 0),
-        0.5 * q0 + 0.25 * pz_q + plus(a_y, 0) + minus(a_y, 0),
-    ]
+    shared = 2.0 * (p + pe)
+    yield evenly(2.0 * (p + pp) + 6.0 * pe, 2.0 * (e + pe) + p + CORNER * pp)
+    yield evenly(shared + pp, 6.0 * e + shared + CORNER * pp)
+    yield evenly(6.0 * p + 2.0 * (pe + pp), 2.0 * (e + p) + pe + CORNER * pp)
+    yield oddly(qe + MIXED * qp)
+    yield evenly(qq, MIXED * qq)
+    yield oddly(q + MIXED * pq)
+
+
+def gradient(get, comp):
+    if comp == Z:
+        qe, qp = odd(get, KEPT), odd(get, SUM)
+        a = 2.0 * qe + 4.0 / 3.0 * qp
+        return 4.0 * qe + 2.0 * qp + plus(a, 0) + minus(a, 0)
+    if comp == X:
+        b = 4.0 * get(KEPT, 0) + 2.0 * (get(SUM, 0) + even(get, KEPT)) + 4.0 / 3.0 * even(get, SUM)
+        return plus(b, 0) - minus(b, 0)
+    q, pq = get(DIFF, 0), even(get, DIFF)
+    a = 2.0 * q + 4.0 / 3.0 * pq
+    return 4.0 * q + 2.0 * pq + plus(a, 0) + minus(a, 0)
 
 
 def poly_dot(first, second, moments):
@@ -174,12 +165,13 @@
 
     def kernel(
         kelvin_in, label_in, patch_in, traits, intensity,
+        warmed_hbm, solution_hbm, residual_hbm,
         warmed_out, solution_out, residual_out,
         temp, label, patch, cond, rate, power, g_row, g_row_back, g_col, g_col_back, g_up, temp_one,
         packs, strips, packed_strain, strain_strips, label_strips,
-        strain, e_label, e_strain, base, field, lanes, stiff,
+        strain, e_label, e_strain, base, beside, field, lanes, stiff,
         sums, sums_a, sums_b, total_a,
-        local_sem, send, recv,
+        local_sem, out_sem, send, recv,
     ):
         gx, gy, gz = lax.axis_index("gx"), lax.axis_index("gy"), lax.axis_index("gz")
         other = 1 - gz
@@ -394,6 +386,8 @@
             return acc
 
         packed_strain[...] = grouped(16, 4, heat_two, jnp.zeros((8, 128), F32))
+        stores = [pltpu.make_async_copy(warmed_out, warmed_hbm, out_sem.at[0])]
+        stores[0].start()
         strains = elastic_sends(strain, lambda dz: 4 * dz, e_strain, packed_strain, strain_strips)
 
         def own_strain(layer, carry):
@@ -409,7 +403,7 @@
 
         largest = jnp.maximum(jnp.maximum(modulus[0], modulus[1]), jnp.maximum(modulus[2], modulus[3]))
         scale = SPAN * largest
-        inverse = 1.0 / jnp.full((1, 128), scale, F32)
+        inverse = 0.125 / jnp.full((1, 128), scale, F32)
         scaled = [m * inverse for m in modulus]
 
         for copy in labels:
@@ -443,51 +437,46 @@
             spread(base, 0, layer, e)
             spread(base, 1, layer, s)
             spread(base, 2, layer, e * s)
+            beside[0, layer], beside[1, layer] = minus(e, 0), plus(e, 0)
             return carry
 
         grouped(12, 2, base_fields, 0)
 
         cuts = [slice(128 * n, 128 * n + 128) for n in range(3)]
 
-        def put(step, layer, chunks):
+        def put(step, layer):
             e = base[0, 0, layer + 1]
+            slot = (step % 2) * 5
             for comp in range(3):
-                value = jnp.concatenate(chunks[comp], axis=1)
-                if step == 3:
-                    field[step, comp, layer + 1, 0:16, 0:256] = value[0:16]
-                else:
-                    field[step, comp, layer + 1] = value
-                    ahead, behind = plus(value, 1), minus(value, 1)
-                    slot = (step % 2) * 5
-                    lanes[slot, comp, layer + 1] = ahead + behind
-                    lanes[slot + 1, comp, layer + 1] = ahead - behind
-                    value = e * value
-                    ahead, behind = plus(value, 1), minus(value, 1)
-                    lanes[slot + 2, comp, layer + 1] = value
-                    lanes[slot + 3, comp, layer + 1] = ahead + behind
-                    lanes[slot + 4, comp, layer + 1] = ahead - behind
+                value = field[step, comp, layer + 1]
+                ahead, behind = plus(value, 1), minus(value, 1)
+                lanes[slot, comp, layer + 1] = ahead + behind
+                lanes[slot + 1, comp, layer + 1] = ahead - behind
+                value = e * value
+                ahead, behind = plus(value, 1), minus(value, 1)
+                lanes[slot + 2, comp, layer + 1] = value
+                lanes[slot + 3, comp, layer + 1] = ahead + behind
+                lanes[slot + 4, comp, layer + 1] = ahead - behind
 
         def first_vector(layer, carry):
-            chunks = [[], [], []]
             for cut in cuts:
                 def get(n):
                     return lambda kind, dz: base[n, kind, layer + 1 + dz, :, cut]
 
                 e, s = base[0, 0, layer + 1, :, cut], base[1, 0, layer + 1, :, cut]
-                inside = e > 0.0
-                de, ds, des = gradient(get(0)), gradient(get(1)), gradient(get(2))
                 for comp in range(3):
-                    load = -(e * ds[comp] + s * de[comp] + des[comp])
-                    chunks[comp].append(jnp.where(inside, load, 0.0))
+                    load = -(e * gradient(get(1), comp) + s * gradient(get(0), comp) + gradient(get(2), comp))
+                    field[0, comp, layer + 1, :, cut] = jnp.where(e > 0.0, load, 0.0)
                 for n, value in enumerate(scalar_stencils(get(0))):
-                    stiff[n, layer, :, cut] = value
-            put(0, layer, chunks)
+                    stiff[n, layer, :, cut] = value + (8.0 * DIAGONAL * e - TAU) if n < 3 else value
+            put(0, layer)
             return carry
 
         lax.fori_loop(0, 11, first_vector, 0)
 
+        places = ((0, 3, 4), (3, 1, 5), (4, 5, 2))
+
         def next_vector(step, layer):
-            chunks = [[], [], []]
             slot = (step % 2) * 5
             for cut in cuts if step < 2 else cuts[:2]:
                 def plain(comp, kind, dz):
@@ -498,20 +487,22 @@
                 def weighted(comp, kind, dz):
                     return lanes[slot + 2 + kind, comp, layer + 1 + dz, :, cut]
 
-                ku, kw = stencil(plain), stencil(weighted)
-                e = base[0, 0, layer + 1, :, cut]
-                inside = e > 0.0
-                zz, xx, yy, zx, zy, xy = [stiff[n, layer, :, cut] for n in range(6)]
-                u = [plain(comp, 0, 0) for comp in range(3)]
-                gu = [
-                    zz * u[0] + zx * u[1] + zy * u[2],
-                    zx * u[0] + xx * u[1] + xy * u[2],
-                    zy * u[0] + xy * u[1] + yy * u[2],
-                ]
                 for comp in range(3):
-                    value = e * (DIAGONAL * u[comp] - ku[comp]) + gu[comp] - kw[comp] - TAU * u[comp]
-                    chunks[comp].append(jnp.where(inside, value, 0.0))
-            put(step + 1, layer, chunks)
+                    c, a, b = stencil(plain, comp)
+                    c_w, a_w, b_w = stencil(weighted, comp)
+                    e = base[0, 0, layer + 1, :, cut]
+                    value = -(e * c + c_w)
+                    for n in range(3):
+                        value = value + stiff[places[comp][n], layer, :, cut] * field[step, n, layer + 1, :, cut]
+                    value = value - plus(beside[0, layer, :, cut] * (a + b) + (a_w + b_w), 0)
+                    value = value - minus(beside[1, layer, :, cut] * (a - b) + (a_w - b_w), 0)
+                    value = jnp.where(e > 0.0, value, 0.0)
+                    if step < 2:
+                        field[step + 1, comp, layer + 1, :, cut] = value
+                    else:
+                        field[step + 1, comp, layer + 1, 0:16, cut] = value[0:16]
+            if step < 2:
+                put(step + 1, layer)
 
         for step in range(3):
             def body(layer, carry, step=step):
@@ -570,6 +561,12 @@
             return carry
 
         lax.fori_loop(0, 8, outputs, 0)
+        stores.append(pltpu.make_async_copy(solution_out, solution_hbm, out_sem.at[1]))
+        stores.append(pltpu.make_async_copy(residual_out, residual_hbm, out_sem.at[2]))
+        for copy in stores[1:]:
+            copy.start()
+        for copy in stores:
+            copy.wait()
 
         for copy in heat + labels + strains + first + second:
             copy.wait_send()
@@ -578,11 +575,16 @@
 
 
 def copy_out(*refs):
-    sems = refs[-1]
-    copies = [pltpu.make_async_copy(refs[n], refs[n + 3], sems.at[n]) for n in range(3)]
-    for copy in copies:
+    sources, targets, held, (arrived, left) = refs[:3], refs[3:6], refs[6:9], refs[9:]
+    pieces = [(n, n_piece) for n in (1, 2) for n_piece in range(3)] + [(0, slice(0, 16))]
+    loads = [pltpu.make_async_copy(sources[n].at[k], held[n].at[k], arrived.at[i]) for i, (n, k) in enumerate(pieces)]
+    stores = [pltpu.make_async_copy(held[n].at[k], targets[n].at[k], left.at[i]) for i, (n, k) in enumerate(pieces)]
+    for copy in loads:
         copy.start()
-    for copy in copies:
+    for load, store in zip(loads, stores):
+        load.wait()
+        store.start()
+    for copy in stores:
         copy.wait()
 
 
@@ -590,7 +592,6 @@
     sizes = dict(mesh.shape)
     hbm = pl.BlockSpec(memory_space=pltpu.HBM)
     smem = pl.BlockSpec(memory_space=pltpu.SMEM)
-    vmem = pl.BlockSpec(memory_space=pltpu.VMEM)
     copies = 12 + 11 + 11 + (2 * sizes["gx"] - 1) + (sizes["gy"] - 1)
 
     def per_device(kelvin, label, patch, traits, intensity):
@@ -607,16 +608,18 @@
             make_kernel(sizes),
             out_shape=shapes,
             in_specs=[hbm, hbm, hbm, smem, smem],
-            out_specs=(vmem, vmem, vmem),
+            out_specs=(hbm, hbm, hbm),
             scratch_shapes=[
+                *(pltpu.VMEM(shape.shape, F32) for shape in shapes),
                 heat(), heat(kind=jnp.int32), heat(kind=jnp.int32),
                 heat(17), heat(), heat(), heat(), heat(), heat(), heat(), heat(17), heat(),
                 block(2, 2), block(2, 3, 2), block(), block(2, 3), block(2, 3),
                 pltpu.VMEM((16, 16, 128), F32),
                 pltpu.VMEM((12, 24, 384), jnp.int32), wide(12),
-                wide(3, 3, 13), wide(4, 3, 13), wide(10, 3, 13), wide(6, 11),
+                wide(3, 3, 13), wide(2, 12), wide(4, 3, 13), wide(10, 3, 13), wide(6, 11),
                 row(), row(2 * sizes["gx"] - 1), row(sizes["gy"] - 1), row(),
                 pltpu.SemaphoreType.DMA((4,)),
+                pltpu.SemaphoreType.DMA((3,)),
                 pltpu.SemaphoreType.DMA((copies,)),
                 pltpu.SemaphoreType.DMA((copies,)),
             ],
@@ -627,9 +630,14 @@
         return pl.pallas_call(
             copy_out,
             out_shape=shapes,
-            in_specs=[vmem, vmem, vmem],
+            in_specs=[hbm, hbm, hbm],
             out_specs=(hbm, hbm, hbm),
-            scratch_shapes=[pltpu.SemaphoreType.DMA((3,))],
+            scratch_shapes=[
+                *(pltpu.VMEM(shape.shape, F32) for shape in shapes),
+                pltpu.SemaphoreType.DMA((7,)),
+                pltpu.SemaphoreType.DMA((7,)),
+            ],
+            compiler_params=pltpu.CompilerParams(vmem_limit_bytes=60 * 1024 * 1024),
         )(*results)
 
     columns = P(None, "gx", ("gy", "gz"))

time: 55.4 us -> 54.4 us (0.982)
  Pallas kernels: 54.6 us -> 53.6 us
    pallas_call x1, Pallas kernels: 52.4 us -> 51.6 us  [per_device(): pl.pallas_call(make_kernel(sizes), out_shape=shapes, in_specs=[hbm, hbm,...]
where the time goes in v3:
time: 54.4 us; the launch traced here: 54.2 us
  Pallas kernels  53.6 us (99%)
  between operations  0.64 us (1%)
    pallas_call x1, Pallas kernels, per_device(): pl.pallas_call(make_kernel(sizes), out_shape=shapes, in_specs=[hbm, hbm,...  51.6 us
    pallas_call x1, Pallas kernels, per_device(): pl.pallas_call(copy_out, out_shape=shapes, in_specs=[hbm, hbm, hbm], out_...  2.03 us

profile of v3, /device:TPU:1, one launch (start us, length us, event | category | flops | bytes accessed | tf_op | source)
XLA Modules:
  0.0 54.2 jit_solution(12053313412618093153)
XLA Ops:
  0.6 51.6 %shard_map.76 = (f32[16,16,128]{2,1,0:T(8,128)}, f32[3,8,16,256]{3,2,1,0:T(8,128)}, f32[3,8,16,256]{3,2,1,0:T(8,128)}) custom-call(f32[16,16,128]{2,1,0:T(8,128)} %kelvin_in.1, s32[16,16,128]{2,1,0:T(8,128)} %label_in.1, s32[16,16,128]{2,1,0:T(8,128)} %patch_in.1, f32[4,4]{1,0:T(4,128)} %traits.1, f32[16]{0:T(128)} %intensity.1), custom_call_target="tpu_custom_call" | custom-call | tf_op jit(solution)/shard_map/pallas_call | solution.py:607
  52.2 2.0 %shard_map.77 = (f32[16,16,128]{2,1,0:T(8,128)}, f32[3,8,16,256]{3,2,1,0:T(8,128)}, f32[3,8,16,256]{3,2,1,0:T(8,128)}) custom-call(f32[16,16,128]{2,1,0:T(8,128)} %get-tuple-element.6.refs_0_, f32[3,8,16,256]{3,2,1,0:T(8,128)} %get-tuple-element.7.refs_1_, f32[3,8,16,256]{3,2,1,0:T(8,128)} %get-tuple-element.8.refs_2_), custom_call_target="tpu_custom_call" | custom-call | tf_op jit(solution)/shard_map/pallas_call | solution.py:630

commit v4 on v3

--- a/solution.py
+++ b/solution.py
@@ -169,7 +169,7 @@
         warmed_out, solution_out, residual_out,
         temp, label, patch, cond, rate, power, g_row, g_row_back, g_col, g_col_back, g_up, temp_one,
         packs, strips, packed_strain, strain_strips, label_strips,
-        strain, e_label, e_strain, base, beside, field, lanes, stiff,
+        strain, e_label, e_strain, base, beside, field, lanes_even, lanes_odd, stiff,
         sums, sums_a, sums_b, total_a,
         local_sem, out_sem, send, recv,
     ):
@@ -344,7 +344,7 @@
                 power[layer, :, cut] = lookup(tile_ids[n], tiles)
             return carry
 
-        grouped(16, 4, heat_fields, 0)
+        grouped(16, 8, heat_fields, 0)
         cond[16] = jnp.zeros((24, 256), F32)
 
         def conductances(layer, carry):
@@ -356,7 +356,7 @@
             return carry
 
         g_up[0] = jnp.zeros((24, 256), F32)
-        grouped(16, 4, conductances, 0)
+        grouped(16, 8, conductances, 0)
 
         def heat_step(source, layer):
             own = source[layer]
@@ -370,7 +370,7 @@
             temp_one[layer] = heat_step(temp, layer)
             return carry
 
-        grouped(16, 4, heat_one, 0)
+        grouped(16, 8, heat_one, 0)
 
         start = jnp.where(gz == 0, 0, 124)
 
@@ -385,7 +385,7 @@
                 acc = jnp.where((lane >> 2) == slot, moved, acc)
             return acc
 
-        packed_strain[...] = grouped(16, 4, heat_two, jnp.zeros((8, 128), F32))
+        packed_strain[...] = grouped(16, 8, heat_two, jnp.zeros((8, 128), F32))
         stores = [pltpu.make_async_copy(warmed_out, warmed_hbm, out_sem.at[0])]
         stores[0].start()
         strains = elastic_sends(strain, lambda dz: 4 * dz, e_strain, packed_strain, strain_strips)
@@ -396,7 +396,10 @@
 
         lax.fori_loop(0, 12, own_strain, 0)
 
-        for ref in (base, field, lanes):
+        lanes = (lanes_even, lanes_odd)
+        for n in range(4):
+            beside[n, 0] = jnp.zeros((24, 384), F32)
+        for ref in (base, field, *lanes):
             for n in range(ref.shape[0]):
                 for m in range(ref.shape[1]):
                     ref[n, m, 0] = jnp.zeros((24, 384), F32)
@@ -416,12 +419,6 @@
 
         def stacked(layer):
             return jnp.where(gz == 0, layer, 11 - layer)
-
-        def spread(ref, n, layer, value):
-            ahead, behind = plus(value, 1), minus(value, 1)
-            ref[n, 0, layer + 1] = value
-            ref[n, 1, layer + 1] = ahead + behind
-            ref[n, 2, layer + 1] = ahead - behind
 
         def base_fields(layer, carry):
             raw = stacked(layer)
@@ -434,75 +431,93 @@
             hot = [jnp.where(e_ok[n], hot[n], 0.0) for n in range(3)]
             e = jnp.concatenate(stiffness, axis=1)
             s = jnp.concatenate(hot, axis=1)
-            spread(base, 0, layer, e)
-            spread(base, 1, layer, s)
-            spread(base, 2, layer, e * s)
-            beside[0, layer], beside[1, layer] = minus(e, 0), plus(e, 0)
+            base[0, KEPT, layer + 1], base[1, KEPT, layer + 1] = e, s
             return carry
 
-        grouped(12, 2, base_fields, 0)
+        grouped(12, 4, base_fields, 0)
 
         cuts = [slice(128 * n, 128 * n + 128) for n in range(3)]
 
-        def put(step, layer):
+        def put(step, layer, comps=range(3)):
             e = base[0, 0, layer + 1]
-            slot = (step % 2) * 5
-            for comp in range(3):
+            to = lanes[step % 2]
+            for comp in comps:
                 value = field[step, comp, layer + 1]
                 ahead, behind = plus(value, 1), minus(value, 1)
-                lanes[slot, comp, layer + 1] = ahead + behind
-                lanes[slot + 1, comp, layer + 1] = ahead - behind
-                value = e * value
-                ahead, behind = plus(value, 1), minus(value, 1)
-                lanes[slot + 2, comp, layer + 1] = value
-                lanes[slot + 3, comp, layer + 1] = ahead + behind
-                lanes[slot + 4, comp, layer + 1] = ahead - behind
+                to[0, comp, layer + 1] = ahead + behind
+                to[1, comp, layer + 1] = ahead - behind
+                ahead, behind = beside[2, layer + 1] * ahead, beside[3, layer + 1] * behind
+                to[2, comp, layer + 1] = e * value
+                to[3, comp, layer + 1] = ahead + behind
+                to[4, comp, layer + 1] = ahead - behind
+
+        def spread(layer):
+            e, s = base[0, KEPT, layer + 1], base[1, KEPT, layer + 1]
+            beside[0, layer + 1], beside[1, layer + 1] = minus(e, 0), plus(e, 0)
+            e_ahead, e_behind, s_ahead, s_behind = plus(e, 1), minus(e, 1), plus(s, 1), minus(s, 1)
+            beside[2, layer + 1], beside[3, layer + 1] = e_ahead, e_behind
+            base[2, KEPT, layer + 1] = e * s
+            pairs = ((e_ahead, e_behind), (s_ahead, s_behind), (e_ahead * s_ahead, e_behind * s_behind))
+            for n, (ahead, behind) in enumerate(pairs):
+                base[n, SUM, layer + 1], base[n, DIFF, layer + 1] = ahead + behind, ahead - behind
 
         def first_vector(layer, carry):
-            for cut in cuts:
-                def get(n):
-                    return lambda kind, dz: base[n, kind, layer + 1 + dz, :, cut]
-
-                e, s = base[0, 0, layer + 1, :, cut], base[1, 0, layer + 1, :, cut]
-                for comp in range(3):
-                    load = -(e * gradient(get(1), comp) + s * gradient(get(0), comp) + gradient(get(2), comp))
-                    field[0, comp, layer + 1, :, cut] = jnp.where(e > 0.0, load, 0.0)
-                for n, value in enumerate(scalar_stencils(get(0))):
+            spread(layer + 2)
+            put(0, layer - 1, [2])
+
+            def get(n, cut):
+                return lambda kind, dz: base[n, kind, layer + 1 + dz, :, cut]
+
+            for comp in range(3):
+                for cut in cuts:
+                    e, s = base[0, 0, layer + 1, :, cut], base[1, 0, layer + 1, :, cut]
+                    load = e * gradient(get(1, cut), comp) + s * gradient(get(0, cut), comp) + gradient(get(2, cut), comp)
+                    field[0, comp, layer + 1, :, cut] = jnp.where(e > 0.0, -load, 0.0)
+                if comp < 2:
+                    put(0, layer, [comp])
+                cut = cuts[comp]
+                e = base[0, 0, layer + 1, :, cut]
+                for n, value in enumerate(scalar_stencils(get(0, cut))):
                     stiff[n, layer, :, cut] = value + (8.0 * DIAGONAL * e - TAU) if n < 3 else value
-            put(0, layer)
             return carry
 
+        base[0, KEPT, 13] = base[1, KEPT, 13] = jnp.zeros((24, 384), F32)
+        spread(0)
+        spread(1)
         lax.fori_loop(0, 11, first_vector, 0)
+        put(0, 10, [2])
 
         places = ((0, 3, 4), (3, 1, 5), (4, 5, 2))
 
         def next_vector(step, layer):
-            slot = (step % 2) * 5
-            for cut in cuts if step < 2 else cuts[:2]:
-                def plain(comp, kind, dz):
-                    if kind == 0:
-                        return field[step, comp, layer + 1 + dz, :, cut]
-                    return lanes[slot + kind - 1, comp, layer + 1 + dz, :, cut]
-
-                def weighted(comp, kind, dz):
-                    return lanes[slot + 2 + kind, comp, layer + 1 + dz, :, cut]
-
-                for comp in range(3):
+            held = lanes[step % 2]
+            if step < 2:
+                put(step + 1, layer - 1, [2])
+            for comp in range(3):
+                for cut in cuts if step < 2 else cuts[:2]:
+                    def plain(comp, kind, dz):
+                        if kind == 0:
+                            return field[step, comp, layer + 1 + dz, :, cut]
+                        return held[kind - 1, comp, layer + 1 + dz, :, cut]
+
+                    def weighted(comp, kind, dz):
+                        return held[2 + kind, comp, layer + 1 + dz, :, cut]
+
                     c, a, b = stencil(plain, comp)
                     c_w, a_w, b_w = stencil(weighted, comp)
                     e = base[0, 0, layer + 1, :, cut]
                     value = -(e * c + c_w)
                     for n in range(3):
                         value = value + stiff[places[comp][n], layer, :, cut] * field[step, n, layer + 1, :, cut]
-                    value = value - plus(beside[0, layer, :, cut] * (a + b) + (a_w + b_w), 0)
-                    value = value - minus(beside[1, layer, :, cut] * (a - b) + (a_w - b_w), 0)
+                    value = value - plus(beside[0, layer + 1, :, cut] * (a + b) + (a_w + b_w), 0)
+                    value = value - minus(beside[1, layer + 1, :, cut] * (a - b) + (a_w - b_w), 0)
                     value = jnp.where(e > 0.0, value, 0.0)
                     if step < 2:
                         field[step + 1, comp, layer + 1, :, cut] = value
                     else:
                         field[step + 1, comp, layer + 1, 0:16, cut] = value[0:16]
-            if step < 2:
-                put(step + 1, layer)
+                if step < 2 and comp < 2:
+                    put(step + 1, layer, [comp])
 
         for step in range(3):
             def body(layer, carry, step=step):
@@ -510,6 +525,8 @@
                 return carry
 
             lax.fori_loop(0, 10 - step, body, 0)
+            if step < 2:
+                put(step + 1, 9 - step, [2])
 
         def products(layer, acc):
             acc = list(acc)
@@ -616,7 +633,7 @@
                 block(2, 2), block(2, 3, 2), block(), block(2, 3), block(2, 3),
                 pltpu.VMEM((16, 16, 128), F32),
                 pltpu.VMEM((12, 24, 384), jnp.int32), wide(12),
-                wide(3, 3, 13), wide(2, 12), wide(4, 3, 13), wide(10, 3, 13), wide(6, 11),
+                wide(3, 3, 14), wide(4, 14), wide(4, 3, 13), wide(5, 3, 13), wide(5, 3, 13), wide(6, 11),
                 row(), row(2 * sizes["gx"] - 1), row(sizes["gy"] - 1), row(),
                 pltpu.SemaphoreType.DMA((4,)),
                 pltpu.SemaphoreType.DMA((3,)),

time: 54.4 us -> 52.1 us (0.958)
  Pallas kernels: 53.6 us -> 51.3 us
    pallas_call x1, Pallas kernels: 51.6 us -> 49.3 us  [per_device(): pl.pallas_call(make_kernel(sizes), out_shape=shapes, in_specs=[hbm, hbm,...]
where the time goes in v4:
time: 52.1 us; the launch traced here: 51.9 us
  Pallas kernels  51.3 us (98%)
  between operations  0.64 us (1%)
    pallas_call x1, Pallas kernels, per_device(): pl.pallas_call(make_kernel(sizes), out_shape=shapes, in_specs=[hbm, hbm,...  49.3 us
    pallas_call x1, Pallas kernels, per_device(): pl.pallas_call(copy_out, out_shape=shapes, in_specs=[hbm, hbm, hbm], out_...  2.03 us

profile of v4, /device:TPU:1, one launch (start us, length us, event | category | flops | bytes accessed | tf_op | source)
XLA Modules:
  0.0 51.9 jit_solution(14048252220006251426)
XLA Ops:
  0.6 49.3 %shard_map.76 = (f32[16,16,128]{2,1,0:T(8,128)}, f32[3,8,16,256]{3,2,1,0:T(8,128)}, f32[3,8,16,256]{3,2,1,0:T(8,128)}) custom-call(f32[16,16,128]{2,1,0:T(8,128)} %kelvin_in.1, s32[16,16,128]{2,1,0:T(8,128)} %label_in.1, s32[16,16,128]{2,1,0:T(8,128)} %patch_in.1, f32[4,4]{1,0:T(4,128)} %traits.1, f32[16]{0:T(128)} %intensity.1), custom_call_target="tpu_custom_call" | custom-call | tf_op jit(solution)/shard_map/pallas_call | solution.py:624
  49.9 2.0 %shard_map.77 = (f32[16,16,128]{2,1,0:T(8,128)}, f32[3,8,16,256]{3,2,1,0:T(8,128)}, f32[3,8,16,256]{3,2,1,0:T(8,128)}) custom-call(f32[16,16,128]{2,1,0:T(8,128)} %get-tuple-element.6.refs_0_, f32[3,8,16,256]{3,2,1,0:T(8,128)} %get-tuple-element.7.refs_1_, f32[3,8,16,256]{3,2,1,0:T(8,128)} %get-tuple-element.8.refs_2_), custom_call_target="tpu_custom_call" | custom-call | tf_op jit(solution)/shard_map/pallas_call | solution.py:647

commit v5 on v4

--- a/solution.py
+++ b/solution.py
@@ -213,6 +213,7 @@
         everyone = peers + ring_a[2:-2] + ring_b[1:-1] if nx > 2 and ny > 2 else peers + ring_a + ring_b
         for peer in everyone:
             pl.semaphore_signal(barrier, inc=1, device_id=peer, device_id_type=MESH)
+
         for copy in loads:
             copy.wait()
 
@@ -279,10 +280,36 @@
                     out.append(remote(pack_src, pack_dst.at[gz, 1 - dx], (nexts[dx], side_gy, dz)))
             return out
 
+        labels = elastic_sends(label, lambda dz: 4 * dz, e_label, packs.at[gz, 0], label_strips)
+
+        materials = range(4)
+        conductivity = [traits[0, m] for m in materials]
+        capacity = [traits[1, m] for m in materials]
+        modulus = [traits[2, m] for m in materials]
+        expansion = [traits[3, m] for m in materials]
+        tiles = [intensity[t] for t in range(16)]
+
+        cond[16] = g_up[0] = jnp.zeros((24, 256), F32)
+        lanes = (lanes_even, lanes_odd)
+        for n in range(4):
+            beside[n, 0] = jnp.zeros((24, 384), F32)
+        for ref in (base, field, *lanes):
+            for n in range(ref.shape[0]):
+                for m in range(ref.shape[1]):
+                    ref[n, m, 0] = jnp.zeros((24, 384), F32)
+        base[0, KEPT, 13] = base[1, KEPT, 13] = jnp.zeros((24, 384), F32)
+
+        def own_fields(layer, carry):
+            ids = label[layer, 0:16, 0:128]
+            cond[layer, 0:16, 0:128] = lookup(ids, conductivity)
+            rate[layer, 0:16, 0:128] = TIME_STEP / lookup(ids, capacity)
+            power[layer, 0:16, 0:128] = lookup(patch[layer, 0:16, 0:128], tiles)
+            return carry
+
+        grouped(16, 8, own_fields, 0)
+
         for copy in heat:
             copy.wait_recv()
-
-        labels = elastic_sends(label, lambda dz: 4 * dz, e_label, packs.at[gz, 0], label_strips)
 
         def halo_blocks(blocks, inset=0, last=252):
             right = [blocks(0, d) for d in (-1, 0, 1)]
@@ -320,32 +347,24 @@
         right_limit = jnp.where(last_tile, 0, 64)
         left_limit = jnp.where(first_tile, 128, 64)
         cols_ok = (wide_lane < right_limit) | (wide_lane >= left_limit)
-        grid_ok = [rows_ok, rows_ok & cols_ok]
+        grid_ok = [rows_ok[16:24], rows_ok & cols_ok]
         e_right_limit = jnp.where(gy == ny - 1, 0, 64)
         e_left_limit = jnp.where(gy == 0, 128, 64)
         e_cols_ok = (wide_lane < e_right_limit) | (wide_lane >= e_left_limit)
         e_ok = [rows_ok, rows_ok, rows_ok & e_cols_ok]
 
-        materials = range(4)
-        conductivity = [traits[0, m] for m in materials]
-        capacity = [traits[1, m] for m in materials]
-        modulus = [traits[2, m] for m in materials]
-        expansion = [traits[3, m] for m in materials]
-        tiles = [intensity[t] for t in range(16)]
-
         def heat_fields(layer, carry):
             temp[layer, :, 128:256] = temp_halo(layer)
-            ids = [label[layer, :, 0:128], label_halo(layer).astype(jnp.int32)]
-            tile_ids = [patch[layer, :, 0:128], patch_halo(layer).astype(jnp.int32)]
-            for n in range(2):
-                cut = slice(128 * n, 128 * n + 128)
-                cond[layer, :, cut] = jnp.where(grid_ok[n], lookup(ids[n], conductivity), 0.0)
-                rate[layer, :, cut] = TIME_STEP / lookup(ids[n], capacity)
-                power[layer, :, cut] = lookup(tile_ids[n], tiles)
+            places = ((slice(16, 24), slice(0, 128)), (slice(0, 24), slice(128, 256)))
+            ids = [label[layer, 16:24, 0:128], label_halo(layer).astype(jnp.int32)]
+            tile_ids = [patch[layer, 16:24, 0:128], patch_halo(layer).astype(jnp.int32)]
+            for (rows, columns), own, tile, inside in zip(places, ids, tile_ids, grid_ok):
+                cond[layer, rows, columns] = jnp.where(inside, lookup(own, conductivity), 0.0)
+                rate[layer, rows, columns] = TIME_STEP / lookup(own, capacity)
+                power[layer, rows, columns] = lookup(tile, tiles)
             return carry
 
         grouped(16, 8, heat_fields, 0)
-        cond[16] = jnp.zeros((24, 256), F32)
 
         def conductances(layer, carry):
             own = cond[layer]
@@ -355,7 +374,6 @@
             g_up[layer + 1] = conduct(own, cond[layer + 1])
             return carry
 
-        g_up[0] = jnp.zeros((24, 256), F32)
         grouped(16, 8, conductances, 0)
 
         def heat_step(source, layer):
@@ -396,14 +414,6 @@
 
         lax.fori_loop(0, 12, own_strain, 0)
 
-        lanes = (lanes_even, lanes_odd)
-        for n in range(4):
-            beside[n, 0] = jnp.zeros((24, 384), F32)
-        for ref in (base, field, *lanes):
-            for n in range(ref.shape[0]):
-                for m in range(ref.shape[1]):
-                    ref[n, m, 0] = jnp.zeros((24, 384), F32)
-
         largest = jnp.maximum(jnp.maximum(modulus[0], modulus[1]), jnp.maximum(modulus[2], modulus[3]))
         scale = SPAN * largest
         inverse = 0.125 / jnp.full((1, 128), scale, F32)
@@ -411,32 +421,58 @@
 
         for copy in labels:
             copy.wait_recv()
+
+        e_label_halo = halo_blocks(lambda side, d: label_strips[side, d + 1])
+
+        def stacked(layer):
+            return jnp.where(gz == 0, layer, 11 - layer)
+
+        cuts = [slice(128 * n, 128 * n + 128) for n in range(3)]
+
+        def modulus_fields(layer, carry):
+            raw = stacked(layer)
+            ids = [e_label[raw, :, cuts[0]], e_label[raw, :, cuts[1]], e_label_halo(raw + 4 * gz).astype(jnp.int32)]
+            for n, cut in enumerate(cuts):
+                base[0, KEPT, layer + 1, :, cut] = jnp.where(e_ok[n], lookup(ids[n], scaled), 0.0)
+            return carry
+
+        grouped(12, 4, modulus_fields, 0)
+
+        def spread_modulus(layer):
+            e = base[0, KEPT, layer + 1]
+            beside[0, layer + 1], beside[1, layer + 1] = minus(e, 0), plus(e, 0)
+            ahead, behind = plus(e, 1), minus(e, 1)
+            beside[2, layer + 1], beside[3, layer + 1] = ahead, behind
+            base[0, SUM, layer + 1], base[0, DIFF, layer + 1] = ahead + behind, ahead - behind
+
+        def get_base(n, layer, cut):
+            return lambda kind, dz: base[n, kind, layer + 1 + dz, :, cut]
+
+        def stiffness(layer, carry):
+            spread_modulus(layer + 2)
+            for cut in cuts:
+                e = base[0, KEPT, layer + 1, :, cut]
+                for n, value in enumerate(scalar_stencils(get_base(0, layer, cut))):
+                    stiff[n, layer, :, cut] = value + (8.0 * DIAGONAL * e - TAU) if n < 3 else value
+            return carry
+
+        spread_modulus(0)
+        spread_modulus(1)
+        lax.fori_loop(0, 10, stiffness, 0)
+
         for copy in strains:
             copy.wait_recv()
 
-        e_label_halo = halo_blocks(lambda side, d: label_strips[side, d + 1])
         e_strain_halo = halo_blocks(lambda side, d: strain_strips[side, d + 1])
 
-        def stacked(layer):
-            return jnp.where(gz == 0, layer, 11 - layer)
-
-        def base_fields(layer, carry):
+        def strain_fields(layer, carry):
             raw = stacked(layer)
-            ids = [e_label[raw, :, 0:128], e_label[raw, :, 128:256]]
-            hot = [e_strain[raw, :, 0:128], e_strain[raw, :, 128:256]]
-            whole = raw + 4 * gz
-            ids.append(e_label_halo(whole).astype(jnp.int32))
-            hot.append(e_strain_halo(whole))
-            stiffness = [jnp.where(e_ok[n], lookup(ids[n], scaled), 0.0) for n in range(3)]
-            hot = [jnp.where(e_ok[n], hot[n], 0.0) for n in range(3)]
-            e = jnp.concatenate(stiffness, axis=1)
-            s = jnp.concatenate(hot, axis=1)
-            base[0, KEPT, layer + 1], base[1, KEPT, layer + 1] = e, s
-            return carry
-
-        grouped(12, 4, base_fields, 0)
-
-        cuts = [slice(128 * n, 128 * n + 128) for n in range(3)]
+            hot = [e_strain[raw, :, cuts[0]], e_strain[raw, :, cuts[1]], e_strain_halo(raw + 4 * gz)]
+            for n, cut in enumerate(cuts):
+                base[1, KEPT, layer + 1, :, cut] = jnp.where(e_ok[n], hot[n], 0.0)
+            return carry
+
+        grouped(12, 4, strain_fields, 0)
 
         def put(step, layer, comps=range(3)):
             e = base[0, 0, layer + 1]
@@ -451,39 +487,29 @@
                 to[3, comp, layer + 1] = ahead + behind
                 to[4, comp, layer + 1] = ahead - behind
 
-        def spread(layer):
-            e, s = base[0, KEPT, layer + 1], base[1, KEPT, layer + 1]
-            beside[0, layer + 1], beside[1, layer + 1] = minus(e, 0), plus(e, 0)
-            e_ahead, e_behind, s_ahead, s_behind = plus(e, 1), minus(e, 1), plus(s, 1), minus(s, 1)
-            beside[2, layer + 1], beside[3, layer + 1] = e_ahead, e_behind
-            base[2, KEPT, layer + 1] = e * s
-            pairs = ((e_ahead, e_behind), (s_ahead, s_behind), (e_ahead * s_ahead, e_behind * s_behind))
-            for n, (ahead, behind) in enumerate(pairs):
-                base[n, SUM, layer + 1], base[n, DIFF, layer + 1] = ahead + behind, ahead - behind
+        def spread_strain(layer):
+            s = base[1, KEPT, layer + 1]
+            ahead, behind = plus(s, 1), minus(s, 1)
+            base[2, KEPT, layer + 1] = base[0, KEPT, layer + 1] * s
+            base[1, SUM, layer + 1], base[1, DIFF, layer + 1] = ahead + behind, ahead - behind
+            ahead, behind = beside[2, layer + 1] * ahead, beside[3, layer + 1] * behind
+            base[2, SUM, layer + 1], base[2, DIFF, layer + 1] = ahead + behind, ahead - behind
 
         def first_vector(layer, carry):
-            spread(layer + 2)
+            spread_strain(layer + 2)
             put(0, layer - 1, [2])
-
-            def get(n, cut):
-                return lambda kind, dz: base[n, kind, layer + 1 + dz, :, cut]
-
             for comp in range(3):
                 for cut in cuts:
-                    e, s = base[0, 0, layer + 1, :, cut], base[1, 0, layer + 1, :, cut]
-                    load = e * gradient(get(1, cut), comp) + s * gradient(get(0, cut), comp) + gradient(get(2, cut), comp)
+                    of_e, of_s, of_es = [gradient(get_base(n, layer, cut), comp) for n in range(3)]
+                    e, s = base[0, KEPT, layer + 1, :, cut], base[1, KEPT, layer + 1, :, cut]
+                    load = e * of_s + s * of_e + of_es
                     field[0, comp, layer + 1, :, cut] = jnp.where(e > 0.0, -load, 0.0)
                 if comp < 2:
                     put(0, layer, [comp])
-                cut = cuts[comp]
-                e = base[0, 0, layer + 1, :, cut]
-                for n, value in enumerate(scalar_stencils(get(0, cut))):
-                    stiff[n, layer, :, cut] = value + (8.0 * DIAGONAL * e - TAU) if n < 3 else value
-            return carry
-
-        base[0, KEPT, 13] = base[1, KEPT, 13] = jnp.zeros((24, 384), F32)
-        spread(0)
-        spread(1)
+            return carry
+
+        spread_strain(0)
+        spread_strain(1)
         lax.fori_loop(0, 11, first_vector, 0)
         put(0, 10, [2])
 

time: 52.1 us -> 50.4 us (0.967)
  Pallas kernels: 51.3 us -> 49.6 us
    pallas_call x1, Pallas kernels: 49.3 us -> 47.6 us  [per_device(): pl.pallas_call(make_kernel(sizes), out_shape=shapes, in_specs=[hbm, hbm,...]
where the time goes in v5:
time: 50.4 us; the launch traced here: 50.3 us
  Pallas kernels  49.6 us (98%)
  between operations  0.64 us (1%)
    pallas_call x1, Pallas kernels, per_device(): pl.pallas_call(make_kernel(sizes), out_shape=shapes, in_specs=[hbm, hbm,...  47.6 us
    pallas_call x1, Pallas kernels, per_device(): pl.pallas_call(copy_out, out_shape=shapes, in_specs=[hbm, hbm, hbm], out_...  2.03 us

profile of v5, /device:TPU:1, one launch (start us, length us, event | category | flops | bytes accessed | tf_op | source)
XLA Modules:
  0.0 50.3 jit_solution(1601852836661335299)
XLA Ops:
  0.6 47.6 %shard_map.76 = (f32[16,16,128]{2,1,0:T(8,128)}, f32[3,8,16,256]{3,2,1,0:T(8,128)}, f32[3,8,16,256]{3,2,1,0:T(8,128)}) custom-call(f32[16,16,128]{2,1,0:T(8,128)} %kelvin_in.1, s32[16,16,128]{2,1,0:T(8,128)} %label_in.1, s32[16,16,128]{2,1,0:T(8,128)} %patch_in.1, f32[4,4]{1,0:T(4,128)} %traits.1, f32[16]{0:T(128)} %intensity.1), custom_call_target="tpu_custom_call" | custom-call | tf_op jit(solution)/shard_map/pallas_call | solution.py:650
  48.2 2.0 %shard_map.77 = (f32[16,16,128]{2,1,0:T(8,128)}, f32[3,8,16,256]{3,2,1,0:T(8,128)}, f32[3,8,16,256]{3,2,1,0:T(8,128)}) custom-call(f32[16,16,128]{2,1,0:T(8,128)} %get-tuple-element.6.refs_0_, f32[3,8,16,256]{3,2,1,0:T(8,128)} %get-tuple-element.7.refs_1_, f32[3,8,16,256]{3,2,1,0:T(8,128)} %get-tuple-element.8.refs_2_), custom_call_target="tpu_custom_call" | custom-call | tf_op jit(solution)/shard_map/pallas_call | solution.py:673

commit v6 on v5

--- a/solution.py
+++ b/solution.py
@@ -205,12 +205,18 @@
             if not (dx == 0 and dy is gy and dz is gz)
         ]
         number_a = gx * 2 + gz
-        ring_a = []
-        for step in range(1, group_a):
+
+
+        def farthest_first(size):
+            return sorted(range(1, size), key=lambda step: abs(size // 2 - step))
+
+        ring_a, ring_b = {}, {}
+        for step in farthest_first(group_a):
             there = lax.rem(number_a + step, group_a)
-            ring_a.append((there // 2, gy, lax.rem(there, 2)))
-        ring_b = [(gx, lax.rem(gy + step, ny), gz) for step in range(1, group_b)]
-        everyone = peers + ring_a[2:-2] + ring_b[1:-1] if nx > 2 and ny > 2 else peers + ring_a + ring_b
+            ring_a[step] = (there // 2, gy, lax.rem(there, 2))
+        for step in farthest_first(group_b):
+            ring_b[step] = (gx, lax.rem(gy + step, ny), gz)
+        everyone = peers + [ring_a[step] for step in range(3, group_a - 2)] + [ring_b[step] for step in range(2, group_b - 1)]
         for peer in everyone:
             pl.semaphore_signal(barrier, inc=1, device_id=peer, device_id_type=MESH)
 
@@ -257,27 +263,29 @@
             return copy
 
         heat = []
+        right_gy = jnp.where(gz == 0, gy, gy_up)
+        left_gy = jnp.where(gz == 0, gy_down, gy)
+        for dx in (-1, 1, 0):
+            rows = {0: slice(0, 8), -1: slice(0, 2), 1: slice(6, 8)}[dx]
+            for side, there in ((0, left_gy), (1, right_gy)):
+                heat.append(remote(packs.at[side, :, rows], strips.at[side, 1 - dx, :, rows], (nexts[dx], there, other)))
         for ref, deep in ((temp, 2), (label, 2), (patch, 1)):
             up, down = slice(16 - deep, 16), slice(24 - deep, 24)
             heat.append(remote(ref.at[:, 0:deep, 0:128], ref.at[:, 16 : 16 + deep, 0:128], (nexts[-1], gy, gz)))
             heat.append(remote(ref.at[:, up, 0:128], ref.at[:, down, 0:128], (nexts[1], gy, gz)))
-        right_gy = jnp.where(gz == 0, gy, gy_up)
-        left_gy = jnp.where(gz == 0, gy_down, gy)
-        for dx in (0, -1, 1):
-            rows = {0: slice(0, 8), -1: slice(0, 2), 1: slice(6, 8)}[dx]
-            for side, there in ((0, left_gy), (1, right_gy)):
-                heat.append(remote(packs.at[side, :, rows], strips.at[side, 1 - dx, :, rows], (nexts[dx], there, other)))
 
         side_gy = jnp.where(gz == 0, gy_down, gy_up)
 
         def elastic_sends(src, src_layers, dst, pack_src, pack_dst):
-            out = [remote(src.at[pl.ds(src_layers(other), 12), 0:16, 0:128], dst.at[:, 0:16, own_lanes], (gx, gy, other))]
-            for dz in (gz, other):
+            out = []
+            for dx in (1, -1, 0):
+                for dz in (other, gz):
+                    out.append(remote(pack_src, pack_dst.at[gz, 1 - dx], (nexts[dx], side_gy, dz)))
+            for dz in (other, gz):
                 layers = pl.ds(src_layers(dz), 12)
                 out.append(remote(src.at[layers, 0:4, 0:128], dst.at[:, 16:20, own_lanes], (nexts[-1], gy, dz)))
                 out.append(remote(src.at[layers, 12:16, 0:128], dst.at[:, 20:24, own_lanes], (nexts[1], gy, dz)))
-                for dx in (0, -1, 1):
-                    out.append(remote(pack_src, pack_dst.at[gz, 1 - dx], (nexts[dx], side_gy, dz)))
+            out.append(remote(src.at[pl.ds(src_layers(other), 12), 0:16, 0:128], dst.at[:, 0:16, own_lanes], (gx, gy, other)))
             return out
 
         labels = elastic_sends(label, lambda dz: 4 * dz, e_label, packs.at[gz, 0], label_strips)
@@ -575,7 +583,7 @@
         sums[...] = jnp.sum(jnp.where(lane == sub, mine, 0.0), axis=0, keepdims=True)
 
         def reduce_over(ring, src, dst):
-            copies = [remote(src, dst.at[n], peer) for n, peer in enumerate(ring)]
+            copies = [remote(src, dst.at[n], peer) for n, peer in enumerate(ring.values())]
             for copy in copies:
                 copy.wait_recv()
             value = src[...]
@@ -593,21 +601,20 @@
         r_of = [jnp.broadcast_to(c * scale, (16, 256)) for c in r_of]
         sign = jnp.where(gz == 0, 1.0, -1.0)
 
-        def outputs(layer, carry):
-            place = jnp.where(gz == 0, layer, 7 - layer)
-            for comp in range(3):
+        for comp in range(3):
+            def outputs(layer, carry, comp=comp):
+                place = jnp.where(gz == 0, layer, 7 - layer)
                 v = [field[step, comp, layer + 1, 0:16, 0:256] for step in range(4)]
                 x = x_of[0] * v[0] + x_of[1] * v[1] + x_of[2] * v[2]
                 r = r_of[0] * v[0] + r_of[1] * v[1] + r_of[2] * v[2] + r_of[3] * v[3]
                 solution_out[comp, place] = x * sign if comp == 0 else x
                 residual_out[comp, place] = r * sign if comp == 0 else r
-            return carry
-
-        lax.fori_loop(0, 8, outputs, 0)
-        stores.append(pltpu.make_async_copy(solution_out, solution_hbm, out_sem.at[1]))
-        stores.append(pltpu.make_async_copy(residual_out, residual_hbm, out_sem.at[2]))
-        for copy in stores[1:]:
-            copy.start()
+                return carry
+
+            grouped(8, 2, outputs, 0)
+            for n, (held, there) in enumerate(((solution_out, solution_hbm), (residual_out, residual_hbm))):
+                stores.append(pltpu.make_async_copy(held.at[comp], there.at[comp], out_sem.at[1 + 2 * comp + n]))
+                stores[-1].start()
         for copy in stores:
             copy.wait()
 
@@ -662,7 +669,7 @@
                 wide(3, 3, 14), wide(4, 14), wide(4, 3, 13), wide(5, 3, 13), wide(5, 3, 13), wide(6, 11),
                 row(), row(2 * sizes["gx"] - 1), row(sizes["gy"] - 1), row(),
                 pltpu.SemaphoreType.DMA((4,)),
-                pltpu.SemaphoreType.DMA((3,)),
+                pltpu.SemaphoreType.DMA((7,)),
                 pltpu.SemaphoreType.DMA((copies,)),
                 pltpu.SemaphoreType.DMA((copies,)),
             ],

time: 50.4 us -> 49.3 us (0.978)
  Pallas kernels: 49.6 us -> 48.5 us
    pallas_call x1, Pallas kernels: 47.6 us -> 46.5 us  [per_device(): pl.pallas_call(make_kernel(sizes), out_shape=shapes, in_specs=[hbm, hbm,...]
where the time goes in v6:
time: 49.3 us; the launch traced here: 49.1 us
  Pallas kernels  48.5 us (98%)
  between operations  0.64 us (1%)
    pallas_call x1, Pallas kernels, per_device(): pl.pallas_call(make_kernel(sizes), out_shape=shapes, in_specs=[hbm, hbm,...  46.5 us
    pallas_call x1, Pallas kernels, per_device(): pl.pallas_call(copy_out, out_shape=shapes, in_specs=[hbm, hbm, hbm], out_...  2.03 us

profile of v6, /device:TPU:1, one launch (start us, length us, event | category | flops | bytes accessed | tf_op | source)
XLA Modules:
  0.0 49.1 jit_solution(2863341533026662464)
XLA Ops:
  0.6 46.5 %shard_map.76 = (f32[16,16,128]{2,1,0:T(8,128)}, f32[3,8,16,256]{3,2,1,0:T(8,128)}, f32[3,8,16,256]{3,2,1,0:T(8,128)}) custom-call(f32[16,16,128]{2,1,0:T(8,128)} %kelvin_in.1, s32[16,16,128]{2,1,0:T(8,128)} %label_in.1, s32[16,16,128]{2,1,0:T(8,128)} %patch_in.1, f32[4,4]{1,0:T(4,128)} %traits.1, f32[16]{0:T(128)} %intensity.1), custom_call_target="tpu_custom_call" | custom-call | tf_op jit(solution)/shard_map/pallas_call | solution.py:657
  47.1 2.0 %shard_map.77 = (f32[16,16,128]{2,1,0:T(8,128)}, f32[3,8,16,256]{3,2,1,0:T(8,128)}, f32[3,8,16,256]{3,2,1,0:T(8,128)}) custom-call(f32[16,16,128]{2,1,0:T(8,128)} %get-tuple-element.6.refs_0_, f32[3,8,16,256]{3,2,1,0:T(8,128)} %get-tuple-element.7.refs_1_, f32[3,8,16,256]{3,2,1,0:T(8,128)} %get-tuple-element.8.refs_2_), custom_call_target="tpu_custom_call" | custom-call | tf_op jit(solution)/shard_map/pallas_call | solution.py:680

commit v7 on v6

--- a/solution.py
+++ b/solution.py
@@ -164,9 +164,9 @@
     group_a, group_b = nx * 2, ny
 
     def kernel(
-        kelvin_in, label_in, patch_in, traits, intensity,
+        kelvin_in, label_in, patch_in, traits_in, intensity_in,
         warmed_hbm, solution_hbm, residual_hbm,
-        warmed_out, solution_out, residual_out,
+        traits, intensity, warmed_out, solution_out, residual_out,
         temp, label, patch, cond, rate, power, g_row, g_row_back, g_col, g_col_back, g_up, temp_one,
         packs, strips, packed_strain, strain_strips, label_strips,
         strain, e_label, e_strain, base, beside, field, lanes_even, lanes_odd, stiff,
@@ -186,6 +186,8 @@
             pltpu.make_async_copy(
                 label_in.at[pl.ds(4 * gz, 12)], e_label.at[:, 0:16, own_lanes], local_sem.at[3]
             ),
+            pltpu.make_async_copy(traits_in, traits, local_sem.at[4]),
+            pltpu.make_async_copy(intensity_in, intensity, local_sem.at[5]),
         ]
         for copy in loads:
             copy.start()
@@ -294,7 +296,7 @@
         conductivity = [traits[0, m] for m in materials]
         capacity = [traits[1, m] for m in materials]
         modulus = [traits[2, m] for m in materials]
-        expansion = [traits[3, m] for m in materials]
+        expansion = [-traits[3, m] for m in materials]
         tiles = [intensity[t] for t in range(16)]
 
         cond[16] = g_up[0] = jnp.zeros((24, 256), F32)
@@ -511,7 +513,7 @@
                     of_e, of_s, of_es = [gradient(get_base(n, layer, cut), comp) for n in range(3)]
                     e, s = base[0, KEPT, layer + 1, :, cut], base[1, KEPT, layer + 1, :, cut]
                     load = e * of_s + s * of_e + of_es
-                    field[0, comp, layer + 1, :, cut] = jnp.where(e > 0.0, -load, 0.0)
+                    field[0, comp, layer + 1, :, cut] = jnp.where(e > 0.0, load, 0.0)
                 if comp < 2:
                     put(0, layer, [comp])
             return carry
@@ -540,9 +542,8 @@
                     c, a, b = stencil(plain, comp)
                     c_w, a_w, b_w = stencil(weighted, comp)
                     e = base[0, 0, layer + 1, :, cut]
-                    value = -(e * c + c_w)
-                    for n in range(3):
-                        value = value + stiff[places[comp][n], layer, :, cut] * field[step, n, layer + 1, :, cut]
+                    terms = [stiff[places[comp][n], layer, :, cut] * field[step, n, layer + 1, :, cut] for n in range(3)]
+                    value = terms[0] + terms[1] + terms[2] - (e * c + c_w)
                     value = value - plus(beside[0, layer + 1, :, cut] * (a + b) + (a_w + b_w), 0)
                     value = value - minus(beside[1, layer + 1, :, cut] * (a - b) + (a_w - b_w), 0)
                     value = jnp.where(e > 0.0, value, 0.0)
@@ -641,7 +642,6 @@
 def solution(mesh):
     sizes = dict(mesh.shape)
     hbm = pl.BlockSpec(memory_space=pltpu.HBM)
-    smem = pl.BlockSpec(memory_space=pltpu.SMEM)
     copies = 12 + 11 + 11 + (2 * sizes["gx"] - 1) + (sizes["gy"] - 1)
 
     def per_device(kelvin, label, patch, traits, intensity):
@@ -657,9 +657,10 @@
         results = pl.pallas_call(
             make_kernel(sizes),
             out_shape=shapes,
-            in_specs=[hbm, hbm, hbm, smem, smem],
+            in_specs=[hbm] * 5,
             out_specs=(hbm, hbm, hbm),
             scratch_shapes=[
+                pltpu.SMEM(traits.shape, F32), pltpu.SMEM(intensity.shape, F32),
                 *(pltpu.VMEM(shape.shape, F32) for shape in shapes),
                 heat(), heat(kind=jnp.int32), heat(kind=jnp.int32),
                 heat(17), heat(), heat(), heat(), heat(), heat(), heat(), heat(17), heat(),
@@ -668,7 +669,7 @@
                 pltpu.VMEM((12, 24, 384), jnp.int32), wide(12),
                 wide(3, 3, 14), wide(4, 14), wide(4, 3, 13), wide(5, 3, 13), wide(5, 3, 13), wide(6, 11),
                 row(), row(2 * sizes["gx"] - 1), row(sizes["gy"] - 1), row(),
-                pltpu.SemaphoreType.DMA((4,)),
+                pltpu.SemaphoreType.DMA((6,)),
                 pltpu.SemaphoreType.DMA((7,)),
                 pltpu.SemaphoreType.DMA((copies,)),
                 pltpu.SemaphoreType.DMA((copies,)),

time: 49.3 us -> 48.5 us (0.984)
  Pallas kernels: 48.5 us -> 47.8 us
    pallas_call x1, Pallas kernels: 46.5 us -> 45.7 us  [per_device(): pl.pallas_call(make_kernel(sizes), out_shape=shapes, in_specs=[hbm] * 5,...]
where the time goes in v7:
time: 48.5 us; the launch traced here: 48.4 us
  Pallas kernels  47.8 us (99%)
  between operations  0.64 us (1%)
    pallas_call x1, Pallas kernels, per_device(): pl.pallas_call(make_kernel(sizes), out_shape=shapes, in_specs=[hbm] * 5,...  45.7 us
    pallas_call x1, Pallas kernels, per_device(): pl.pallas_call(copy_out, out_shape=shapes, in_specs=[hbm, hbm, hbm], out_...  2.03 us

profile of v7, /device:TPU:1, one launch (start us, length us, event | category | flops | bytes accessed | tf_op | source)
XLA Modules:
  0.0 48.4 jit_solution(7564170381631458376)
XLA Ops:
  0.6 45.7 %shard_map.76 = (f32[16,16,128]{2,1,0:T(8,128)}, f32[3,8,16,256]{3,2,1,0:T(8,128)}, f32[3,8,16,256]{3,2,1,0:T(8,128)}) custom-call(f32[16,16,128]{2,1,0:T(8,128)} %kelvin_in.1, s32[16,16,128]{2,1,0:T(8,128)} %label_in.1, s32[16,16,128]{2,1,0:T(8,128)} %patch_in.1, f32[4,4]{1,0:T(4,128)} %traits_in.1, f32[16]{0:T(128)} %intensity_in.1), custom_call_target="tpu_custom_call" | custom-call | tf_op jit(solution)/shard_map/pallas_call | solution.py:657
  46.4 2.0 %shard_map.77 = (f32[16,16,128]{2,1,0:T(8,128)}, f32[3,8,16,256]{3,2,1,0:T(8,128)}, f32[3,8,16,256]{3,2,1,0:T(8,128)}) custom-call(f32[16,16,128]{2,1,0:T(8,128)} %get-tuple-element.6.refs_0_, f32[3,8,16,256]{3,2,1,0:T(8,128)} %get-tuple-element.7.refs_1_, f32[3,8,16,256]{3,2,1,0:T(8,128)} %get-tuple-element.8.refs_2_), custom_call_target="tpu_custom_call" | custom-call | tf_op jit(solution)/shard_map/pallas_call | solution.py:681

commit v8 on v7

--- a/solution.py
+++ b/solution.py
@@ -222,7 +222,7 @@
         for peer in everyone:
             pl.semaphore_signal(barrier, inc=1, device_id=peer, device_id_type=MESH)
 
-        for copy in loads:
+        for copy in loads[:3]:
             copy.wait()
 
         lane = lax.broadcasted_iota(jnp.int32, (8, 128), 1)
@@ -246,7 +246,7 @@
                     acc[2 * side + 1] = jnp.where((place >= 2) & (place < 4), moved, acc[2 * side + 1])
             return tuple(acc)
 
-        packed = grouped(16, 8, pack_inputs, tuple(jnp.zeros((8, 128), F32) for _ in range(4)))
+        packed = grouped(16, 16, pack_inputs, tuple(jnp.zeros((8, 128), F32) for _ in range(4)))
         for k in range(4):
             packs[k // 2, k % 2] = packed[k]
 
@@ -291,6 +291,9 @@
             return out
 
         labels = elastic_sends(label, lambda dz: 4 * dz, e_label, packs.at[gz, 0], label_strips)
+
+        for copy in loads[3:]:
+            copy.wait()
 
         materials = range(4)
         conductivity = [traits[0, m] for m in materials]

time: 48.5 us -> 48.5 us (level)
  no operation moved by 1% of the time
where the time goes in v8:
time: 48.5 us; the launch traced here: 48.4 us
  Pallas kernels  47.7 us (98%)
  between operations  0.64 us (1%)
    pallas_call x1, Pallas kernels, per_device(): pl.pallas_call(make_kernel(sizes), out_shape=shapes, in_specs=[hbm] * 5,...  45.7 us
    pallas_call x1, Pallas kernels, per_device(): pl.pallas_call(copy_out, out_shape=shapes, in_specs=[hbm, hbm, hbm], out_...  2.03 us

profile of v8, /device:TPU:1, one launch (start us, length us, event | category | flops | bytes accessed | tf_op | source)
XLA Modules:
  0.0 48.4 jit_solution(16646498022962901043)
XLA Ops:
  0.6 45.7 %shard_map.76 = (f32[16,16,128]{2,1,0:T(8,128)}, f32[3,8,16,256]{3,2,1,0:T(8,128)}, f32[3,8,16,256]{3,2,1,0:T(8,128)}) custom-call(f32[16,16,128]{2,1,0:T(8,128)} %kelvin_in.1, s32[16,16,128]{2,1,0:T(8,128)} %label_in.1, s32[16,16,128]{2,1,0:T(8,128)} %patch_in.1, f32[4,4]{1,0:T(4,128)} %traits_in.1, f32[16]{0:T(128)} %intensity_in.1), custom_call_target="tpu_custom_call" | custom-call | tf_op jit(solution)/shard_map/pallas_call | solution.py:660
  46.3 2.0 %shard_map.77 = (f32[16,16,128]{2,1,0:T(8,128)}, f32[3,8,16,256]{3,2,1,0:T(8,128)}, f32[3,8,16,256]{3,2,1,0:T(8,128)}) custom-call(f32[16,16,128]{2,1,0:T(8,128)} %get-tuple-element.6.refs_0_, f32[3,8,16,256]{3,2,1,0:T(8,128)} %get-tuple-element.7.refs_1_, f32[3,8,16,256]{3,2,1,0:T(8,128)} %get-tuple-element.8.refs_2_), custom_call_target="tpu_custom_call" | custom-call | tf_op jit(solution)/shard_map/pallas_call | solution.py:684
